TPU v7x, 32 devices: a 4x4x1 block of a 4x4x8 slice. The times are simulated.
32 devices in a mesh: part: 1 (over z), tp: 4 (over y), ep: 8 (over x, core).
Axes of the slice: x: 4, y: 4, z: 1, core: 2. Of those that a mesh axis runs over, the one named last changes fastest.
The devices are a block of a 4x4x8 slice.
Arguments:
- x_in: bfloat16 [64, 1024, 768], P(('part', 'ep'))
- idx_first: int32 [64, 1024], P(('part', 'ep'))
- idx_second: int32 [64, 1024], P(('part', 'ep'))
- rel_bias: float32 [2, 12, 1024], P(None, 'tp')
- norm_gain: float32 [4, 768], replicated
- attn_qkv: bfloat16 [2, 3, 768, 768], P(None, None, None, 'tp')
- attn_out: bfloat16 [2, 768, 768], P(None, 'tp')
- gate_w: float32 [768, 64], replicated
- expert_w0: bfloat16 [64, 768, 3072], P('ep', None, 'tp')
- expert_w1: bfloat16 [64, 768, 3072], P('ep', None, 'tp')
- expert_down: bfloat16 [64, 3072, 768], P('ep', 'tp')
- dense_w0: bfloat16 [768, 3072], P(None, 'tp')
- dense_w1: bfloat16 [768, 3072], P(None, 'tp')
- dense_down: bfloat16 [3072, 768], P('tp')
Outputs:
- output: bfloat16 [64, 1024, 768], P(('part', 'ep'))
All inputs are finite; a program needn't handle non-finite values.
Results may differ from a plain program's by a relative error of at most 0.02.
Values are sent between devices in bfloat16 or wider.
A program may use at most 768 MiB of HBM per device.

v0:
```python
import jax
import jax.numpy as jnp
from jax import lax
from jax.sharding import PartitionSpec as P


def rms_norm(hidden, gain):
    wide = hidden.astype(jnp.float32)
    scale = lax.rsqrt(jnp.mean(wide * wide, axis=-1, keepdims=True) + 1e-6)
    return (wide * scale * gain).astype(jnp.bfloat16)


def add_residual(base, branch):
    return (base.astype(jnp.float32) + branch.astype(jnp.float32)).astype(jnp.bfloat16)


def causal_bias(rel_table, row_start, rows):
    heads, length = rel_table.shape
    pattern = jnp.concatenate([rel_table[:, :1], jnp.zeros((heads, length), rel_table.dtype), rel_table[:, :0:-1]], axis=1)
    pattern = jnp.roll(pattern, row_start, axis=1)
    flat = jnp.tile(pattern, (1, rows))[:, : rows * (2 * length - 1)]
    table = flat.reshape(heads, rows, 2 * length - 1)[:, :, :length]
    later = jnp.arange(length)[None, :] > (row_start + jnp.arange(rows))[:, None]
    return jnp.where(later[None], -1e30, table)


def route(idx_first, idx_second, gate_probs):
    group_tokens, experts = gate_probs.shape
    capacity = (2 * group_tokens + experts - 1) // experts
    expert_ids = jnp.arange(experts, dtype=jnp.int32)
    hot_first = (idx_first[:, None] == expert_ids).astype(jnp.int32)
    hot_second = (idx_second[:, None] == expert_ids).astype(jnp.int32)
    pos_first = jnp.sum((jnp.cumsum(hot_first, axis=0) - 1) * hot_first, axis=1)
    first_count = jnp.sum(hot_first, axis=0)
    pos_second = jnp.sum((jnp.cumsum(hot_second, axis=0) - 1 + first_count[None, :]) * hot_second, axis=1)
    gate_first = jnp.sum(jnp.where(hot_first == 1, gate_probs, 0.0), axis=1)
    gate_second = jnp.sum(jnp.where(hot_second == 1, gate_probs, 0.0), axis=1)
    total = gate_first + gate_second
    empty = experts * capacity
    slot_first = jnp.where(pos_first < capacity, idx_first * capacity + pos_first, empty)
    slot_second = jnp.where(pos_second < capacity, idx_second * capacity + pos_second, empty)
    return slot_first, slot_second, gate_first / total, gate_second / total


def dispatch(h_flat, slot_first, slot_second, experts):
    group_tokens = h_flat.shape[0]
    capacity = (2 * group_tokens + experts - 1) // experts
    token_ids = jnp.arange(group_tokens, dtype=jnp.int32)
    slot_token = jnp.full((experts * capacity,), group_tokens, jnp.int32)
    slot_token = slot_token.at[jnp.concatenate([slot_first, slot_second])].set(jnp.concatenate([token_ids, token_ids]), mode="drop")
    return jnp.take(h_flat, slot_token, axis=0, mode="fill", fill_value=0)


def combine(expert_rows, slot_first, slot_second, gate_first, gate_second):
    picked_first = jnp.take(expert_rows, slot_first, axis=0, mode="fill", fill_value=0).astype(jnp.float32)
    picked_second = jnp.take(expert_rows, slot_second, axis=0, mode="fill", fill_value=0).astype(jnp.float32)
    return gate_first[:, None] * picked_first + gate_second[:, None] * picked_second


def attend(h_norm, query_norm, qkv_w, rel_table, row_start):
    num_seqs, length = h_norm.shape[:2]
    rows = query_norm.shape[1]
    heads = rel_table.shape[0]
    head_dim = qkv_w.shape[-1] // heads

    def project(source, weight, count):
        proj = jnp.dot(source, weight, preferred_element_type=jnp.float32).astype(jnp.bfloat16)
        return proj.reshape(num_seqs, count, heads, head_dim)

    query_rows = project(query_norm, qkv_w[0], rows)
    key_rows = project(h_norm, qkv_w[1], length)
    value_rows = project(h_norm, qkv_w[2], length)
    logits = jnp.einsum("bqhe,bkhe->bhqk", query_rows, key_rows, preferred_element_type=jnp.float32) * head_dim ** -0.5
    weights = jax.nn.softmax(logits + causal_bias(rel_table, row_start, rows), axis=-1).astype(jnp.bfloat16)
    context = jnp.einsum("bhqk,bkhe->bqhe", weights, value_rows, preferred_element_type=jnp.float32).astype(jnp.bfloat16)
    return context.reshape(num_seqs, rows, heads * head_dim)


def project_out(context, out_w):
    return jnp.dot(context, out_w, preferred_element_type=jnp.float32).astype(jnp.bfloat16)


def dense_ffn(rows, first_w, second_w, down_w):
    hidden = (jax.nn.gelu(jnp.dot(rows, first_w, preferred_element_type=jnp.float32)) * jnp.dot(rows, second_w, preferred_element_type=jnp.float32)).astype(jnp.bfloat16)
    return jnp.dot(hidden, down_w, preferred_element_type=jnp.float32).astype(jnp.bfloat16)


def expert_ffn(tokens, first_w, second_w, down_w):
    gate_act = jnp.einsum("ecd,edf->ecf", tokens, first_w, preferred_element_type=jnp.float32)
    linear = jnp.einsum("ecd,edf->ecf", tokens, second_w, preferred_element_type=jnp.float32)
    hidden = (jax.nn.gelu(gate_act) * linear).astype(jnp.bfloat16)
    return jnp.einsum("ecf,efd->ecd", hidden, down_w, preferred_element_type=jnp.float32).astype(jnp.bfloat16)


def moe_branch(h_norm, gate_w, idx_first, idx_second, expert_w0, expert_w1, expert_down):
    width = h_norm.shape[-1]
    experts = gate_w.shape[1]
    gate_probs = jax.nn.softmax(jnp.dot(h_norm, gate_w, preferred_element_type=jnp.float32), axis=-1)
    slot_first, slot_second, gate_first, gate_second = route(idx_first.reshape(-1), idx_second.reshape(-1), gate_probs)
    send = dispatch(h_norm, slot_first, slot_second, experts).reshape(experts, -1, width)
    received = lax.all_to_all(send, "ep", 0, 1, tiled=True)
    expert_out = expert_ffn(received, expert_w0, expert_w1, expert_down)
    returned = lax.all_to_all(expert_out, "ep", 1, 0, tiled=True).reshape(-1, width)
    return combine(returned, slot_first, slot_second, gate_first, gate_second).astype(jnp.bfloat16)


def solution(mesh):
    row_spec = P(("part", "ep"))
    in_specs = (row_spec, row_spec, row_spec, P(None, "tp"), P(), P(None, None, None, "tp"), P(None, "tp"), P(), P("ep", None, "tp"), P("ep", None, "tp"), P("ep", "tp"), P(None, "tp"), P(None, "tp"), P("tp"))

    def device_step(x_in, idx_first, idx_second, rel_bias, norm_gain, attn_qkv, attn_out, gate_w, expert_w0, expert_w1, expert_down, dense_w0, dense_w1, dense_down):
        num_seqs, length, width = x_in.shape
        h_norm = rms_norm(x_in, norm_gain[0])
        attn_part = project_out(attend(h_norm, h_norm, attn_qkv[0], rel_bias[0], 0), attn_out[0])
        residual = add_residual(x_in, lax.psum(attn_part, "tp"))
        h_norm = rms_norm(residual, norm_gain[1]).reshape(num_seqs * length, width)
        moe_part = moe_branch(h_norm, gate_w, idx_first, idx_second, expert_w0, expert_w1, expert_down)
        residual = add_residual(residual, lax.psum(moe_part, "tp").reshape(num_seqs, length, width))
        h_norm = rms_norm(residual, norm_gain[2])
        attn_part = project_out(attend(h_norm, h_norm, attn_qkv[1], rel_bias[1], 0), attn_out[1])
        residual = add_residual(residual, lax.psum(attn_part, "tp"))
        ffn_part = dense_ffn(rms_norm(residual, norm_gain[3]), dense_w0, dense_w1, dense_down)
        return add_residual(residual, lax.psum(ffn_part, "tp"))

    return jax.shard_map(device_step, mesh=mesh, in_specs=in_specs, out_specs=row_spec, check_vma=False)
```

profile of v0, /device:TPU:97, one launch (start us, length us, event | category | flops | bytes accessed | tf_op | source)
XLA Modules:
  0.0 3342.1 jit_solution(6622322521374470077)
XLA Ops:
  10.5 7.1 fusion.19
  17.7 9.1 fusion.85
  26.8 8.9 fusion.88
  35.7 6.3 fusion.82
  43.0 11.5 broadcast_bitcast_fusion.1
  54.5 33.4 %copy.35 = f32[1,3,1024,2048]{3,1,2,0:T(4,128)} copy(f32[1,3,1024,2048]{3,2,1,0:T(8,128)} %broadcast_bitcast_fusion.1) | data formatting | bytes 50331648
  87.9 22.8 slice_bitcast_fusion.1
  110.7 467.0 %while.2 = (u32[]{:T(128)}, f32[1,3,2096128]{2,1,0:T(4,128)}, f32[6288384]{0:T(1024)}, u32[]{}, f32[]{:T(128)}, /*index=5*/u32[]{}, u32[]{}, u32[]{}) while((u32[]{:T(128)}, f32[1,3,2096128]{2,1,0:T(4,128)}, f32[6288384]{0:T(1024)}, u32[]{}, f32[]{:T(128)}, /*index=5*/u32[]{}, u32[]{}, u32[]{}) %tuple.46), condition=%wide.cond, body=%wide.body.sunk | while | flops 9 | bytes 33538240
  111.4 83.8 %dynamic-slice_reduce_fusion.4 = f32[2096128]{0:T(1024)} fusion(f32[]{:T(128)} %broadcast.281, f32[1,3,2096128]{2,1,0:T(4,128)} %get-tuple-element.139, u32[]{:T(128)S(6)} %multiply.40, u32[]{:T(128)S(6)} %multiply.41), kind=kLoop, calls=%fused_computation.187.clone.1 | loop fusion | bytes 16769036
  195.2 71.2 %dynamic-update-slice.4 = f32[6288384]{0:T(1024)} dynamic-update-slice(f32[6288384]{0:T(1024)} %get-tuple-element.132, f32[2096128]{0:T(1024)} %dynamic-slice_reduce_fusion.4, u32[]{:T(128)S(6)} %add.391) | dynamic-update-slice | bytes 16769028
  267.0 83.8 %dynamic-slice_reduce_fusion.4 = f32[2096128]{0:T(1024)} fusion(f32[]{:T(128)} %broadcast.281, f32[1,3,2096128]{2,1,0:T(4,128)} %get-tuple-element.139, u32[]{:T(128)S(6)} %multiply.40, u32[]{:T(128)S(6)} %multiply.41), kind=kLoop, calls=%fused_computation.187.clone.1 | loop fusion | bytes 16769036
  350.8 71.2 %dynamic-update-slice.4 = f32[6288384]{0:T(1024)} dynamic-update-slice(f32[6288384]{0:T(1024)} %get-tuple-element.132, f32[2096128]{0:T(1024)} %dynamic-slice_reduce_fusion.4, u32[]{:T(128)S(6)} %add.391) | dynamic-update-slice | bytes 16769028
  422.5 83.8 %dynamic-slice_reduce_fusion.4 = f32[2096128]{0:T(1024)} fusion(f32[]{:T(128)} %broadcast.281, f32[1,3,2096128]{2,1,0:T(4,128)} %get-tuple-element.139, u32[]{:T(128)S(6)} %multiply.40, u32[]{:T(128)S(6)} %multiply.41), kind=kLoop, calls=%fused_computation.187.clone.1 | loop fusion | bytes 16769036
  506.4 71.3 %dynamic-update-slice.4 = f32[6288384]{0:T(1024)} dynamic-update-slice(f32[6288384]{0:T(1024)} %get-tuple-element.132, f32[2096128]{0:T(1024)} %dynamic-slice_reduce_fusion.4, u32[]{:T(128)S(6)} %add.391) | dynamic-update-slice | bytes 16769028
  577.7 36.9 %reshape.265 = f32[3,1024,2047]{2,1,0:T(8,128)} reshape(f32[6288384]{0:T(1024)} %get-tuple-element.10) | data formatting | bytes 50307072 | tf_op jit(solution)/shard_map/reshape | solution.py:22
  615.9 11.5 broadcast_bitcast_fusion
  627.4 33.4 %copy.40 = f32[1,3,1024,2048]{3,1,2,0:T(4,128)} copy(f32[1,3,1024,2048]{3,2,1,0:T(8,128)} %broadcast_bitcast_fusion) | data formatting | bytes 50331648
  660.8 22.8 slice_bitcast_fusion
  683.6 467.0 %while.3 = (u32[]{:T(128)}, f32[1,3,2096128]{2,1,0:T(4,128)}, f32[6288384]{0:T(1024)}, u32[]{}, f32[]{:T(128)}, /*index=5*/u32[]{}, u32[]{}, u32[]{}) while((u32[]{:T(128)}, f32[1,3,2096128]{2,1,0:T(4,128)}, f32[6288384]{0:T(1024)}, u32[]{}, f32[]{:T(128)}, /*index=5*/u32[]{}, u32[]{}, u32[]{}) %tuple.43), condition=%wide.cond.1, body=%wide.body.1.sunk | while | flops 9 | bytes 33538240
  684.1 83.9 %dynamic-slice_reduce_fusion.5 = f32[2096128]{0:T(1024)} fusion(f32[]{:T(128)} %broadcast.282, f32[1,3,2096128]{2,1,0:T(4,128)} %get-tuple-element.115, u32[]{:T(128)S(6)} %multiply.44, u32[]{:T(128)S(6)} %multiply.45), kind=kLoop, calls=%fused_computation.188.clone.1 | loop fusion | bytes 16769036
  768.0 71.3 %dynamic-update-slice.5 = f32[6288384]{0:T(1024)} dynamic-update-slice(f32[6288384]{0:T(1024)} %get-tuple-element.108, f32[2096128]{0:T(1024)} %dynamic-slice_reduce_fusion.5, u32[]{:T(128)S(6)} %add.393) | dynamic-update-slice | bytes 16769028
  839.8 83.9 %dynamic-slice_reduce_fusion.5 = f32[2096128]{0:T(1024)} fusion(f32[]{:T(128)} %broadcast.282, f32[1,3,2096128]{2,1,0:T(4,128)} %get-tuple-element.115, u32[]{:T(128)S(6)} %multiply.44, u32[]{:T(128)S(6)} %multiply.45), kind=kLoop, calls=%fused_computation.188.clone.1 | loop fusion | bytes 16769036
  923.7 71.2 %dynamic-update-slice.5 = f32[6288384]{0:T(1024)} dynamic-update-slice(f32[6288384]{0:T(1024)} %get-tuple-element.108, f32[2096128]{0:T(1024)} %dynamic-slice_reduce_fusion.5, u32[]{:T(128)S(6)} %add.393) | dynamic-update-slice | bytes 16769028
  995.4 83.9 %dynamic-slice_reduce_fusion.5 = f32[2096128]{0:T(1024)} fusion(f32[]{:T(128)} %broadcast.282, f32[1,3,2096128]{2,1,0:T(4,128)} %get-tuple-element.115, u32[]{:T(128)S(6)} %multiply.44, u32[]{:T(128)S(6)} %multiply.45), kind=kLoop, calls=%fused_computation.188.clone.1 | loop fusion | bytes 16769036
  1079.3 71.2 %dynamic-update-slice.5 = f32[6288384]{0:T(1024)} dynamic-update-slice(f32[6288384]{0:T(1024)} %get-tuple-element.108, f32[2096128]{0:T(1024)} %dynamic-slice_reduce_fusion.5, u32[]{:T(128)S(6)} %add.393) | dynamic-update-slice | bytes 16769028
  1150.5 37.1 %reshape.274 = f32[3,1024,2047]{2,1,0:T(8,128)} reshape(f32[6288384]{0:T(1024)} %get-tuple-element.15) | data formatting | bytes 50307072 | tf_op jit(solution)/shard_map/reshape | solution.py:22
  1187.7 20.1 slice_select_fusion
  1207.7 12.6 copy.24
  1220.4 46.2 %fusion.147 = (f32[8,3,1024]{2,1,0:T(4,128)S(1)}, f32[8,3,1024,1024]{2,3,1,0:T(8,128)}) fusion(f32[3,1024,1024]{1,2,0:T(8,128)} %copy.24, bf16[8,1024,3,64]{1,3,2,0:T(8,128)(2,1)} %bitcast.169, bf16[8,1024,3,64]{1,3,2,0:T(8,128)(2,1)} %bitcast.170), kind=kOutput, calls=%fused_computation.184 | convolution fusion | flops 3321889792 | bytes 119635968 | tf_op jit(solution)/shard_map/sub | solution.py:74
  1266.6 32.8 fusion.81
  1299.4 6.9 convolution_convert_fusion.1
  1308.0 34.0 %reduce-window.14 = s32[64,64,128]{2,1,0:T(8,128)S(1)} reduce-window(s32[64,64,128]{2,1,0:T(8,128)} %fusion.105, s32[]{:T(128)} %constant.20.clone.1), window={size=1x1x128 pad=0_0x0_0x127_0}, to_apply=%region_9.10 | reduce-window | flops 66584576 | bytes 4194308 | tf_op jit(solution)/shard_map/reduce-window
  1345.6 36.4 %reduce-window.16 = s32[64,64,128]{2,1,0:T(8,128)} reduce-window(s32[64,64,128]{2,1,0:T(8,128)} %fusion.106, s32[]{:T(128)} %constant.20.clone.1), window={size=1x1x128 pad=0_0x0_0x127_0}, to_apply=%region_12.13 | reduce-window | flops 66584576 | bytes 4194308 | tf_op jit(solution)/shard_map/reduce-window.2
  1394.0 60.3 %scatter_custom_fusion = s32[16384]{0:T(1024)S(1)} fusion(s32[16384]{0:T(1024)S(1)} %bitcast.185, s32[16384]{0:T(1024)S(1)} %pad_add_fusion, s32[]{:T(128)} %constant.19.clone.1), kind=kCustom, calls=%fused_computation.159 | custom fusion | bytes 65540 | tf_op jit(solution)/shard_map/scatter | solution.py:50
  1454.4 78.5 %all-reduce.5.cloned.1.call-done = bf16[8,1024,768]{2,1,0:T(8,128)(2,1)} async-done(((bf16[8,1024,768]{2,1,0:T(8,128)(2,1)}), bf16[8,1024,768]{2,1,0:T(8,128)(2,1)}) %all-reduce.5.cloned.1.call-update) | async-done | bytes 12582928 | tf_op jit(solution)/shard_map/psum | solution.py:115
  1532.9 11.1 fusion.23
  1545.0 12.7 fusion.25
  1557.8 79.3 %gather_fusion = bf16[16384,768]{1,0:T(8,128)(2,1)} fusion(bf16[8192,768]{1,0:T(8,128)(2,1)} %bitcast.156, s32[16384]{0:T(1024)S(1)} %fusion.129), kind=kCustom, calls=%fused_computation.2 | custom fusion | bytes 50397184 | tf_op jit(solution)/shard_map/jit(_take)/gather | solution.py:51
  1637.0 17.0 broadcast_select_fusion
  1654.1 278.9 %all_to_all.33 = bf16[64,256,768]{2,1,0:T(8,128)(2,1)S(1)} all-to-all(bf16[64,256,768]{2,1,0:T(8,128)(2,1)} %broadcast_select_fusion), channel_id=1, replica_groups=mesh['part'=1,'tp'=4,'ep'=8] {'ep'}, dimensions={0} | all-to-all | bytes 50331648 | tf_op jit(solution)/shard_map/all_to_all | solution.py:101
  1933.0 8.6 copy.26
  1941.5 34.1 %fusion.150 = f32[8,2048,768]{2,1,0:T(8,128)} fusion(bf16[8,2048,768]{2,1,0:T(8,128)(2,1)} %bitcast.167, bf16[8,768,768]{2,1,0:T(8,128)(2,1)} %param.24), kind=kOutput, calls=%fused_computation.191 | convolution fusion | flops 19327352832 | bytes 84934656 | tf_op jit(solution)/shard_map/ecd,edf->ecf/dot_general | solution.py:89
  1975.7 55.3 %fusion.46 = bf16[8,2048,768]{2,1,0:T(8,128)(2,1)} fusion(bf16[8,768,768]{2,1,0:T(8,128)(2,1)} %param.26, f32[8,2048,768]{2,1,0:T(8,128)} %fusion.150, bf16[8,2048,768]{2,1,0:T(8,128)(2,1)} %bitcast.168, bf16[8,768,768]{2,1,0:T(8,128)(2,1)} %param.25), kind=kOutput, calls=%fused_computation.71 | convolution fusion | flops 38793117696 | bytes 119537664 | tf_op jit(solution)/shard_map/ecf,efd->ecd/dot_general | solution.py:92
  2031.0 26.1 copy.27
  2057.1 8.1 all-to-all-start.1
  2065.3 8.5 fusion.148
  2075.1 263.3 %all-to-all-done.1 = bf16[8,2048,768]{2,0,1:T(8,128)(2,1)} async-done(((bf16[8,2048,768]{2,0,1:T(8,128)(2,1)}), bf16[8,2048,768]{2,0,1:T(8,128)(2,1)}, u32[]{:S(2)}, u32[]{:S(2)}) %all-to-all-start.1) | async-done | bytes 25165856 | tf_op jit(solution)/shard_map/all_to_all | solution.py:103
  2338.4 23.3 copy.28
  2361.7 48.5 %gather_fusion.1 = bf16[8192,768]{1,0:T(8,128)(2,1)} fusion(bf16[16384,768]{1,0:T(8,128)(2,1)} %bitcast.158, s32[8192]{0:T(1024)S(1)} %fusion.132), kind=kCustom, calls=%fused_computation.clone | custom fusion | bytes 25198592 | tf_op jit(solution)/shard_map/jit(_take)/gather | solution.py:55
  2410.2 48.5 %gather_fusion.2 = bf16[8192,768]{1,0:T(8,128)(2,1)} fusion(bf16[16384,768]{1,0:T(8,128)(2,1)} %bitcast.159, s32[8192]{0:T(1024)S(1)} %fusion.133), kind=kCustom, calls=%fused_computation.1.clone | custom fusion | bytes 25198592 | tf_op jit(solution)/shard_map/jit(_take)/gather | solution.py:56
  2458.7 13.4 add_convert_fusion
  2472.2 12.7 copy.29
  2485.0 208.2 %all-reduce.7.cloned.1.call-done = bf16[8,1024,768]{2,1,0:T(8,128)(2,1)} async-done(((bf16[8,1024,768]{2,1,0:T(8,128)(2,1)}), bf16[8,1024,768]{2,1,0:T(8,128)(2,1)}) %all-reduce.7.cloned.1.call-update) | async-done | bytes 12582928 | tf_op jit(solution)/shard_map/psum | solution.py:118
  2693.2 14.2 fusion.27
  2707.4 6.4 fusion.97
  2726.1 46.2 %fusion.149 = (f32[8,3,1024]{2,1,0:T(4,128)S(1)}, f32[8,3,1024,1024]{2,3,1,0:T(8,128)}) fusion(f32[3,1024,1024]{1,2,0:T(8,128)} %copy.29, bf16[8,1024,3,64]{1,3,2,0:T(8,128)(2,1)} %bitcast.172, bf16[8,1024,3,64]{1,3,2,0:T(8,128)(2,1)} %bitcast.171), kind=kOutput, calls=%fused_computation.186 | convolution fusion | flops 3321889792 | bytes 119635968 | tf_op jit(solution)/shard_map/sub | solution.py:74
  2772.4 32.9 fusion.80
  2805.2 6.7 convolution_convert_fusion
  2812.1 222.6 %all-reduce.9.cloned.1.call-done = bf16[8,1024,768]{2,1,0:T(8,128)(2,1)} async-done(((bf16[8,1024,768]{2,1,0:T(8,128)(2,1)}), bf16[8,1024,768]{2,1,0:T(8,128)(2,1)}) %all-reduce.9.cloned.1.call-update) | async-done | bytes 12582928 | tf_op jit(solution)/shard_map/psum | solution.py:121
  3034.7 14.9 fusion.31
  3049.7 17.9 fusion.59
  3067.6 31.0 fusion.61
  3098.7 222.7 %all-reduce.11.cloned.1.call-done = bf16[8,1024,768]{2,1,0:T(8,128)(2,1)} async-done(((bf16[8,1024,768]{2,1,0:T(8,128)(2,1)}), bf16[8,1024,768]{2,1,0:T(8,128)(2,1)}) %all-reduce.11.cloned.1.call-update) | async-done | bytes 12582928 | tf_op jit(solution)/shard_map/psum | solution.py:123
  3321.4 13.9 fusion.34
  (120 shorter events, 41.4 us)
Async XLA Ops:
  6.5 3043.1 %copy-start = (bf16[768,768]{1,0:T(8,128)(2,1)S(1)}, bf16[768,768]{1,0:T(8,128)(2,1)}, u32[]{:S(2)}) copy-start(bf16[768,768]{1,0:T(8,128)(2,1)} %param.27) | copy-start | bytes 3538948
  6.6 11.1 copy-start.22
  6.6 1526.3 %all-reduce.5.cloned.1.call-start = ((), (), s32[]{:S(2)}) async-start(), calls=%async_computation.2 | async-start | bytes 25165824 | tf_op jit(solution)/shard_map/psum | solution.py:115
  17.6 18.1 slice-start
  17.6 18.1 slice-start.1
  26.8 8.9 slice-start.2
  1150.5 37.1 %copy-start.3 = (pred[1024,1024]{1,0:T(8,128)(4,1)S(1)}, pred[1024,1024]{1,0:T(8,128)(4,1)}, u32[]{:S(2)}) copy-start(pred[1024,1024]{1,0:T(8,128)(4,1)} %iota_compare_fusion) | copy-start | bytes 3145732
  1266.6 32.8 copy-start.4
  1299.4 7.0 copy-start.11
  1306.3 37.6 %copy-start.10 = (s32[8,1024]{1,0:T(8,128)S(1)}, s32[8,1024]{1,0:T(8,128)}, u32[]{:S(2)}) copy-start(s32[8,1024]{1,0:T(8,128)} %param.18) | copy-start | bytes 98308
  1385.5 7.9 copy-start.6
  1385.5 7.9 copy-start.8
  1392.7 0.7 copy-start.12
  1393.4 0.6 copy-start.14
  1454.4 89.6 %copy-start.19 = (f32[768]{0:T(1024)S(1)}, f32[768]{0:T(1024)}, u32[]{:S(2)}) copy-start(f32[768]{0:T(1024)} %get-tuple-element.21) | copy-start | bytes 9220
  1532.9 12.1 copy-start.1
  2057.1 8.2 copy-start.15
  2057.1 8.2 copy-start.13
  2057.1 8.2 copy-start.16
  2057.1 281.3 %all-to-all-start.1 = ((bf16[8,2048,768]{2,0,1:T(8,128)(2,1)}), bf16[8,2048,768]{2,0,1:T(8,128)(2,1)}, u32[]{:S(2)}, u32[]{:S(2)}) async-start(bf16[8,2048,768]{2,0,1:T(8,128)(2,1)} %copy.27), calls=%async_computation.1 | async-start | bytes 50331648 | tf_op jit(solution)/shard_map/all_to_all | solution.py:103
  2065.2 9.0 copy-start.7
  2065.2 9.0 copy-start.9
  2065.2 628.0 %all-reduce.7.cloned.1.call-start = ((), (), s32[]{:S(2)}) async-start(), calls=%async_computation.3 | async-start | bytes 25165824 | tf_op jit(solution)/shard_map/psum | solution.py:118
  2410.2 48.5 %copy-start.17 = (pred[8192]{0:T(1024)(128)(4,1)S(1)}, pred[8192]{0:T(1024)(128)(4,1)}, u32[]{:S(2)}) copy-start(pred[8192]{0:T(1024)(128)(4,1)} %get-tuple-element.42) | copy-start | bytes 24580
  2410.2 48.5 %copy-start.18 = (pred[8192]{0:T(1024)(128)(4,1)S(1)}, pred[8192]{0:T(1024)(128)(4,1)}, u32[]{:S(2)}) copy-start(pred[8192]{0:T(1024)(128)(4,1)} %get-tuple-element.40) | copy-start | bytes 24580
  2472.1 562.6 %all-reduce.9.cloned.1.call-start = ((), (), s32[]{:S(2)}) async-start(), calls=%async_computation.4 | async-start | bytes 25165824 | tf_op jit(solution)/shard_map/psum | solution.py:121
  2484.9 222.5 %copy-start.21 = (f32[768]{0:T(1024)S(1)}, f32[768]{0:T(1024)}, u32[]{:S(2)}) copy-start(f32[768]{0:T(1024)} %get-tuple-element.23) | copy-start | bytes 9220
  2485.0 222.5 %copy-start.23 = (bf16[2,3,768,192]{2,3,1,0:T(8,128)(2,1)S(1)}, bf16[2,3,768,192]{2,3,1,0:T(8,128)(2,1)}, u32[]{:S(2)}) copy-start(bf16[2,3,768,192]{2,3,1,0:T(8,128)(2,1)} %param.21) | copy-start | bytes 5308420
  2707.4 12.7 copy-start.2
  2772.3 32.9 copy-start.5
  2812.0 237.7 %copy-start.20 = (f32[768]{0:T(1024)S(1)}, f32[768]{0:T(1024)}, u32[]{:S(2)}) copy-start(f32[768]{0:T(1024)} %get-tuple-element.20) | copy-start | bytes 9220
  2812.0 509.4 %all-reduce.11.cloned.1.call-start = ((), (), s32[]{:S(2)}) async-start(), calls=%async_computation.5 | async-start | bytes 25165824 | tf_op jit(solution)/shard_map/psum | solution.py:123
  3049.7 17.9 copy-start.24
Sparse Core Ops, SparseCore 0:
  1306.5 226.3 all-reduce.4
  2472.3 220.8 all-reduce.6
  2812.1 222.5 all-reduce.8
  3098.8 222.5 all-reduce.10
where the time goes:
time: 3380 us; the launch traced here: 3340 us
  local copies, waits for them, and re-layouts  1470 us (43%)
  waiting for transfers between devices  996 us (29%)
  matrix products  362 us (11%)
  blocking collectives  279 us (8%)
  other arithmetic  209 us (6%)
    unnamed x85, local copies, waits for them, and re-layouts  1070 us
    all_to_all x1, blocking collectives, moe_branch(): received = lax.all_to_all(send, 'ep', 0, 1, tiled=True)  279 us
    all_to_all x1, waiting for transfers between devices, moe_branch(): lax.all_to_all(expert_out, 'ep', 1, 0, tiled=True).reshape(-1, width)  263 us
    psum x1, waiting for transfers between devices, device_step(): return add_residual(residual, lax.psum(ffn_part, 'tp'))  223 us
    psum x1, waiting for transfers between devices, device_step(): residual = add_residual(residual, lax.psum(attn_part, 'tp'))  223 us
    psum x1, waiting for transfers between devices, device_step(): lax.psum(moe_part, 'tp').reshape(num_seqs, length, width)  208 us
    sub x2, matrix products, attend(): jax.nn.softmax(logits + causal_bias(rel_table, row_start, rows), axis=-1)  92.4 us
    gather x1, local copies, waits for them, and re-layouts, dispatch(): return jnp.take(h_flat, slot_token, axis=0, mode='fill', fill_value=0)  79.3 us
  transfers between devices with their start and end apart: 5, of which 5 were waited for; matrix products, arithmetic and copies ran while one was open for 5% of the time, Pallas kernels for 0%

commit v1 on v0

v1 whole, which is shorter than its diff:
```python
import functools

import jax
import jax.numpy as jnp
from jax import lax
from jax.experimental import pallas as pl
from jax.experimental.pallas import tpu as pltpu
from jax.sharding import PartitionSpec as P


F32 = jnp.float32
BF16 = jnp.bfloat16
MASKED = -1e30
VMEM_BYTES = 60 << 20
COLS = 256


def dot(a, b):
    return jnp.dot(a, b, preferred_element_type=F32)


def norm_rows(wide, gain):
    scale = lax.rsqrt(jnp.mean(wide * wide, axis=-1, keepdims=True) + 1e-6)
    return (wide * scale * gain).astype(BF16)


def whole(*shape):
    return pl.BlockSpec(shape, lambda *_: (0,) * len(shape))


def params():
    return pltpu.CompilerParams(vmem_limit_bytes=VMEM_BYTES)


def cost(flops, nbytes):
    return pl.CostEstimate(flops=int(flops), bytes_accessed=int(nbytes), transcendentals=0)


def attention_body(heads, block, head_dim, has_add, *refs):
    x_ref, refs = refs[0], refs[1:]
    if has_add:
        add_ref, refs = refs[0], refs[1:]
    gain_in, gain_out, qkv_w, out_w, rel, res_ref, u_ref, src_s, acc_s, q_s, k_s, v_s, ctx_s, bias_s = refs
    step = pl.program_id(0)
    length = x_ref.shape[0]
    cols = heads * head_dim

    @pl.when(step == 0)
    def _():
        wide = x_ref[...].astype(F32)
        if has_add:
            wide = (wide + add_ref[...].astype(F32)).astype(BF16).astype(F32)
        res_ref[...] = wide.astype(BF16)
        src_s[...] = norm_rows(wide, gain_in[...])
        acc_s[...] = jnp.zeros_like(acc_s)

    source = src_s[...]
    weight = [qkv_w[0, :, n].reshape(source.shape[1], cols) for n in range(3)]
    q_s[...] = dot(source, weight[0]).astype(BF16) * jnp.bfloat16(head_dim ** -0.5)
    k_s[...] = dot(source, weight[1]).astype(BF16)
    v_s[...] = dot(source, weight[2]).astype(BF16)
    lane = lax.broadcasted_iota(jnp.int32, (block, cols), 1)
    span = length + block
    for head in range(heads):
        spread = jnp.broadcast_to(rel[head], (block, span))
        bias_s[head] = pltpu.roll(spread, span - block + 1, 1, stride=1, stride_axis=0)[:, :length]
    for part in range(length // block):
        keys = (part + 1) * block
        rows = pl.ds(part * block, block)
        context = jnp.zeros((block, cols), F32)
        for head in range(heads):
            mine = (lane >= head * head_dim) & (lane < (head + 1) * head_dim)
            query = jnp.where(mine, q_s[rows, :], jnp.bfloat16(0))
            logits = lax.dot_general(query, k_s[:keys, :], (((1,), (1,)), ((), ())), preferred_element_type=F32)
            logits = logits + bias_s[head, :, length - keys:]
            grown = jnp.exp(logits - jnp.max(logits, axis=1, keepdims=True))
            weights = (grown * (1.0 / jnp.sum(grown, axis=1, keepdims=True))).astype(BF16)
            context = jnp.where(mine, dot(weights, v_s[:keys, :]), context)
        ctx_s[rows, :] = context.astype(BF16)
    acc_s[...] += dot(ctx_s[...], out_w[0, 0])

    @pl.when(step == pl.num_programs(0) - 1)
    def _():
        wide = (res_ref[...].astype(F32) + acc_s[...].astype(BF16).astype(F32)).astype(BF16)
        res_ref[...] = wide
        u_ref[...] = norm_rows(wide.astype(F32), gain_out[...])


def attention(x, add, gain_in, gain_out, qkv_w, out_w, layer, rel):
    length, width = x.shape
    parts, peers, _, share, cols = qkv_w.shape
    heads = rel.shape[0] // parts
    block = rel.shape[2] - length
    head_dim = cols // heads
    rows = [x] if add is None else [x, add]
    flops = 2 * length * width * cols * 4 * parts + 4 * length * length * cols * parts * 3
    return pl.pallas_call(
        functools.partial(attention_body, heads, block, head_dim, add is not None),
        grid=(parts,),
        out_shape=[jax.ShapeDtypeStruct((length, width), BF16)] * 2,
        in_specs=[whole(length, width)] * len(rows) + [whole(1, width)] * 2 + [
            pl.BlockSpec((1, peers, 3, share, cols), lambda s: (s, 0, 0, 0, 0)),
            pl.BlockSpec((1, 1, cols, width), lambda s: (s, layer, 0, 0)),
            pl.BlockSpec((heads, 1, length + block), lambda s: (s, 0, 0))],
        out_specs=[whole(length, width)] * 2,
        scratch_shapes=[pltpu.VMEM((length, width), BF16), pltpu.VMEM((length, width), F32)]
        + [pltpu.VMEM((length, cols), BF16)] * 4 + [pltpu.VMEM((heads, block, length), F32)],
        compiler_params=params(),
        cost_estimate=cost(flops, 20e6),
        name="attention",
    )(*rows, gain_in[None], gain_out[None], qkv_w, out_w, rel)


def ffn_quarter(rows, first, second, down, acc_s):
    hidden = down.shape[0]

    def one(n, carry):
        cut = pl.ds(pl.multiple_of(n * COLS, COLS), COLS)
        act = (jax.nn.gelu(dot(rows, first[:, cut])) * dot(rows, second[:, cut])).astype(BF16)
        acc_s[...] += dot(act, down[cut, :])
        return carry

    lax.fori_loop(0, hidden // COLS, one, 0)


def expert_body(me_ref, rows_ref, *refs):
    quarters, out_ref, acc_s = refs[:-2], refs[-2], refs[-1]
    peers, slots, width = rows_ref.shape
    rows = rows_ref[...].reshape(peers * slots, width)
    acc_s[...] = jnp.zeros_like(acc_s)
    for n in range(0, len(quarters), 3):
        ffn_quarter(rows, *[ref.at[0] for ref in quarters[n:n + 3]], acc_s)
    out_ref[...] = acc_s[...].astype(BF16).reshape(out_ref.shape)


def expert(rows, which, me, own, ahead, behind, far):
    peers, slots, width = rows.shape
    count = ahead[0].shape[0]
    step = max(1, peers // 2)
    shapes = [(1, *w.shape[1:]) for w in own]
    at = [lambda s, m: (m[0] * count + which, 0, 0), lambda s, m: (which, 0, 0), lambda s, m: (which, 0, 0), lambda s, m: (0, 0, 0)]
    pieces = (own, ahead, behind, far)
    return pl.pallas_call(
        expert_body,
        grid_spec=pltpu.PrefetchScalarGridSpec(
            num_scalar_prefetch=1,
            grid=(peers // step,),
            in_specs=[pl.BlockSpec((step, slots, width), lambda s, m: (s, 0, 0))]
            + [pl.BlockSpec(shape, index) for index in at for shape in shapes],
            out_specs=pl.BlockSpec((step, slots, width), lambda s, m: (s, 0, 0)),
            scratch_shapes=[pltpu.VMEM((step * slots, width), F32)]),
        out_shape=jax.ShapeDtypeStruct((peers, slots, width), BF16),
        compiler_params=params(),
        cost_estimate=cost(24 * peers * slots * width * own[0].shape[2], 20e6),
        name="expert",
    )(me, rows, *[w for piece in pieces for w in piece])


def dense_body(u_ref, res_ref, first, second, down, out_ref, acc_s):
    acc_s[...] = jnp.zeros_like(acc_s)
    rows = u_ref[...]

    def one(q, carry):
        ffn_quarter(rows, first.at[q], second.at[q], down.at[q], acc_s)
        return carry

    lax.fori_loop(0, first.shape[0], one, 0)
    out_ref[...] = (res_ref[...].astype(F32) + acc_s[...].astype(BF16).astype(F32)).astype(BF16)


def dense(u, res, first, second, down):
    length, width = u.shape
    step = length // 2
    block = pl.BlockSpec((step, width), lambda s: (s, 0))
    return pl.pallas_call(
        dense_body,
        grid=(length // step,),
        out_shape=jax.ShapeDtypeStruct((length, width), BF16),
        in_specs=[block, block, whole(*first.shape), whole(*second.shape), whole(*down.shape)],
        out_specs=block,
        scratch_shapes=[pltpu.VMEM((step, width), F32)],
        compiler_params=params(),
        cost_estimate=cost(6 * length * first.size, 18e6),
        name="dense",
    )(u, res, first, second, down)


def positions(idx_first, idx_second, experts):
    tokens = idx_first.shape[0]
    block = min(256, tokens)
    lane = jnp.arange(2 * experts, dtype=jnp.int32)
    hot = (idx_first[:, None] == lane) | (idx_second[:, None] + experts == lane)
    cells = hot.astype(BF16).reshape(tokens // block, block, 2 * experts)
    lower = jnp.tril(jnp.ones((block, block), BF16))
    within = jnp.einsum("ij,bjn->bin", lower, cells, preferred_element_type=F32)
    totals = within[:, -1, :]
    before = jnp.cumsum(totals, axis=0) - totals
    count = jnp.sum(totals, axis=0)
    shift = jnp.concatenate([jnp.zeros((experts,), F32), count[:experts]]) - 1.0
    ranks = (within + (before + shift)[:, None, :]).reshape(tokens, 2 * experts)
    ranks = jnp.where(hot, ranks, 0.0)
    first = jnp.sum(jnp.where(lane < experts, ranks, 0.0), axis=1)
    second = jnp.sum(jnp.where(lane < experts, 0.0, ranks), axis=1)
    return first.astype(jnp.int32), second.astype(jnp.int32)


def tokens_of_slots(choice, place, owned, capacity):
    number = jnp.arange(1, choice.shape[1] + 1, dtype=jnp.int32)
    number = jnp.concatenate([number, number])
    mine = choice.reshape(-1)[None, :] == owned[:, None]
    high = jnp.where(mine, number // 128, 0).astype(BF16)
    low = jnp.where(mine, number % 128, 0).astype(BF16)
    at_slot = (place.reshape(-1)[:, None] == jnp.arange(capacity, dtype=jnp.int32)).astype(BF16)
    found = dot(jnp.concatenate([high, low]), at_slot).astype(jnp.int32)
    return jnp.maximum(found[: owned.shape[0]] * 128 + found[owned.shape[0]:] - 1, 0)


def pick_body(half, token, *refs):
    chunks, (out0, out1, wide_s, stage_s) = refs[:-4], refs[-4:]
    step = pl.program_id(0)
    block = stage_s.shape[0]

    @pl.when(step == 0)
    def _():
        for n, ref in enumerate(chunks):
            wide_s[n * ref.shape[0]:(n + 1) * ref.shape[0]] = ref[...].astype(F32)

    def eight(n, carry):
        for k in range(8):
            at = n * 8 + k
            stage_s[pl.ds(at, 1), :] = wide_s[pl.ds(token[step * block + at], 1), :]
        return carry

    lax.fori_loop(0, block // 8, eight, 0)

    @pl.when(step < half)
    def _():
        out0[...] = stage_s[...].astype(BF16)

    @pl.when(step >= half)
    def _():
        out1[...] = stage_s[...].astype(BF16)


def pick(chunks, token):
    count = token.shape[0]
    width = chunks[0].shape[1]
    block = min(512, count // 2)
    half = count // 2 // block
    return pl.pallas_call(
        functools.partial(pick_body, half),
        grid=(2 * half,),
        out_shape=[jax.ShapeDtypeStruct((count // 2, width), BF16)] * 2,
        in_specs=[pl.BlockSpec(memory_space=pltpu.SMEM)] + [whole(*c.shape) for c in chunks],
        out_specs=[pl.BlockSpec((block, width), lambda s: (jnp.minimum(s, half - 1), 0)),
                   pl.BlockSpec((block, width), lambda s: (jnp.maximum(s - half, 0), 0))],
        scratch_shapes=[pltpu.VMEM((len(chunks) * chunks[0].shape[0], width), F32), pltpu.VMEM((block, width), F32)],
        compiler_params=params(),
        cost_estimate=cost(20e9, 20e6),
        name="pick",
    )(token, *chunks)


def join_body(half, a_ref, b_ref, out_ref):
    step = pl.program_id(0)

    @pl.when(step < half)
    def _():
        out_ref[...] = a_ref[...]

    @pl.when(step >= half)
    def _():
        out_ref[...] = b_ref[...]


def join(a, b):
    rows, width = a.shape
    block = min(1024, rows)
    half = rows // block
    return pl.pallas_call(
        functools.partial(join_body, half),
        grid=(2 * half,),
        out_shape=jax.ShapeDtypeStruct((2 * rows, width), BF16),
        in_specs=[pl.BlockSpec((block, width), lambda s: (jnp.minimum(s, half - 1), 0)),
                  pl.BlockSpec((block, width), lambda s: (jnp.maximum(s - half, 0), 0))],
        out_specs=pl.BlockSpec((block, width), lambda s: (s, 0)),
        compiler_params=params(),
        cost_estimate=cost(5e9, 25e6),
        name="join",
    )(a, b)


def combine_body(r1, r2, g1, g2, y0, y1, out_ref, wide_s, stage_s):
    step = pl.program_id(0)
    rows = y0.shape[0]
    block = out_ref.shape[0]

    @pl.when(step == 0)
    def _():
        wide_s[:rows] = y0[...].astype(F32)
        wide_s[rows:2 * rows] = y1[...].astype(F32)
        wide_s[2 * rows:] = jnp.zeros_like(wide_s[2 * rows:])

    def eight(n, carry):
        for k in range(8):
            at = n * 8 + k
            t = step * block + at
            stage_s[pl.ds(at, 1), :] = g1[t] * wide_s[pl.ds(r1[t], 1), :] + g2[t] * wide_s[pl.ds(r2[t], 1), :]
        return carry

    lax.fori_loop(0, block // 8, eight, 0)
    out_ref[...] = stage_s[...].astype(BF16)


def combine(rows, gates, y0, y1):
    tokens = rows[0].shape[0]
    width = y0.shape[1]
    block = min(512, tokens)
    smem = pl.BlockSpec(memory_space=pltpu.SMEM)
    return pl.pallas_call(
        combine_body,
        grid=(tokens // block,),
        out_shape=jax.ShapeDtypeStruct((tokens, width), BF16),
        in_specs=[smem] * 4 + [whole(*y0.shape)] * 2,
        out_specs=pl.BlockSpec((block, width), lambda s: (s, 0)),
        scratch_shapes=[pltpu.VMEM((2 * y0.shape[0] + 8, width), F32), pltpu.VMEM((block, width), F32)],
        compiler_params=params(),
        cost_estimate=cost(20e9, 20e6),
        name="combine",
    )(*rows, *gates, y0, y1)


def solution(mesh):
    row_spec = P(("part", "ep"))
    in_specs = (row_spec, row_spec, row_spec, P(None, "tp"), P(), P(None, None, None, "tp"), P(None, "tp"), P(), P("ep", None, "tp"), P("ep", None, "tp"), P("ep", "tp"), P(None, "tp"), P(None, "tp"), P("tp"))
    tp, ep = mesh.shape["tp"], mesh.shape["ep"]
    up = [(d, (d + 1) % tp) for d in range(tp)]
    back = [(d, (d - 1) % tp) for d in range(tp)]

    def device_step(x_in, idx_first, idx_second, rel_bias, norm_gain, attn_qkv, attn_out, gate_w, expert_w0, expert_w1, expert_down, dense_w0, dense_w1, dense_down):
        num_seqs, length, width = x_in.shape
        experts = gate_w.shape[1]
        tokens = num_seqs * length
        capacity = (2 * tokens + experts - 1) // experts
        me, spot = lax.axis_index("tp"), lax.axis_index("ep")
        chunks = num_seqs // tp
        layers = attn_qkv.shape[0]
        held = experts // ep
        count = held // tp
        block = min(256, length)

        def gather_all(piece):
            return lax.all_gather(piece, ("tp", "ep"), axis=0, tiled=False)

        def gather_rows(weight):
            rows = weight.shape[0] // ep
            return lax.dynamic_slice_in_dim(weight, spot * rows, rows, 0)

        share = width // ep
        cols = attn_qkv.shape[3]
        split = ep // layers
        out_piece = lax.dynamic_slice(attn_out, (spot // split, spot % split * (cols // split), 0), (1, cols // split, width))[0]
        qkv_piece = [lax.dynamic_slice(attn_qkv, (n, 0, spot * share, 0), (1, 3, share, cols))[0] for n in range(layers)]
        dense_piece = [gather_rows(w) for w in (dense_w0, dense_w1, dense_down)]
        out_w = gather_all(out_piece).reshape(tp, layers, cols, width)
        qkv_0 = gather_all(qkv_piece[0]).reshape(tp, ep, 3, share, cols)
        rel = lax.all_gather(rel_bias, "tp", axis=1, tiled=True)[:, :, None, ::-1]
        rel = jnp.concatenate([rel, jnp.full((*rel.shape[:3], block), MASKED, F32)], axis=3)

        expert_w = (expert_w0, expert_w1, expert_down)

        def pieces(owner):
            return [lax.dynamic_slice_in_dim(w, owner * count, count, 0) for w in expert_w]

        near = [pieces((me + 1) % tp), pieces((me - 1) % tp)]
        far = [[w[n:n + 1] for w in pieces((me + 2) % tp)] for n in range(count)]
        late = (qkv_piece[1], dense_piece)
        near, far, rel = lax.optimization_barrier((near, far, rel))

        far = [[lax.ppermute(w, "tp", (up, back)[n % 2]) for w in far[n]] for n in range(count)]
        from_behind = [lax.ppermute(w, "tp", up) for w in near[0]]
        from_ahead = [lax.ppermute(w, "tp", back) for w in near[1]]
        qkv_1 = gather_all(late[0]).reshape(tp, ep, 3, share, cols)
        dense_w = [gather_all(w).reshape(tp, *full.shape) for w, full in zip(late[1], (dense_w0, dense_w1, dense_down))]

        res, sent = [], []
        for c in range(chunks):
            x = lax.dynamic_index_in_dim(x_in, c * tp + me, 0, keepdims=False)
            r, u = attention(x, None, norm_gain[0], norm_gain[1], qkv_0, out_w, 0, rel[0])
            res.append(r)
            sent.append(lax.all_gather(u, "tp", axis=0, tiled=True))
        sent, far = lax.optimization_barrier((sent, far))
        far = [[lax.ppermute(w, "tp", (up, back)[n % 2]) for w in far[n]] for n in range(count)]

        first_idx, second_idx, _ = lax.optimization_barrier((idx_first.reshape(-1), idx_second.reshape(-1), u))
        place = positions(first_idx, second_idx, experts)
        owned = (jnp.arange(count, dtype=jnp.int32)[:, None] + me * count + jnp.arange(ep, dtype=jnp.int32) * held).reshape(-1)
        slot_token = tokens_of_slots(jnp.stack([first_idx, second_idx]), jnp.stack(place), owned, capacity).reshape(-1)

        send = pick(sent, slot_token)
        recv = [lax.all_to_all(send[e].reshape(ep, capacity, width), "ep", 0, 0, tiled=True) for e in range(count)]
        recv[0], qkv_1, dense_w = lax.optimization_barrier((recv[0], qkv_1, dense_w))

        lane = jnp.arange(experts, dtype=jnp.int32)
        probs = [jax.nn.softmax(jnp.dot(u, gate_w, preferred_element_type=F32), axis=-1) for u in sent]
        none = count * ep * capacity
        span = tp * length
        rows, gates = [[], []], []
        for c in range(chunks):
            cut = slice(c * span, (c + 1) * span)
            both = [jnp.sum(jnp.where(idx[cut, None] == lane, probs[c], 0.0), axis=1) for idx in (first_idx, second_idx)]
            total = both[0] + both[1]
            gates.append([g / total for g in both])
            for n, idx in enumerate((first_idx[cut], second_idx[cut])):
                local = idx % held
                slot = place[n][cut]
                mine = (slot < capacity) & (local // count == me)
                rows[c].append(jnp.where(mine, (local % count) * (ep * capacity) + idx // held * capacity + slot, none))

        me_ref = me.astype(jnp.int32)[None]
        returned = []
        for e in range(count):
            y = expert(recv[e], e, me_ref, expert_w, from_behind, from_ahead, far[e])
            returned.append(lax.all_to_all(y, "ep", 0, 0, tiled=True).reshape(ep * capacity, width))

        outs = []
        for c in range(chunks):
            part = combine(rows[c], gates[c], *returned)
            mixed = lax.psum_scatter(part, "tp", scatter_dimension=0, tiled=True)
            r, u = attention(res[c], mixed, norm_gain[2], norm_gain[3], qkv_1, out_w, 1, rel[1])
            out = dense(u, r, *dense_w)
            outs.append(lax.all_gather(out, "tp", axis=0, tiled=True))
        return join(*outs).reshape(num_seqs, length, width)

    return jax.shard_map(device_step, mesh=mesh, in_specs=in_specs, out_specs=row_spec, check_vma=False)
```

time: 3380 us -> 1050 us (0.31)
  local copies, waits for them, and re-layouts: 1470 us -> 42.1 us
  waiting for transfers between devices: 996 us -> 493 us
  Pallas kernels: 0 us -> 407 us
  matrix products: 362 us -> 23.4 us
  blocking collectives: 279 us -> 12.3 us
  other arithmetic: 209 us -> 12.1 us
    unnamed x85 -> x67, local copies, waits for them, and re-layouts: 1070 us -> 11 us
    psum x4 -> x0, waiting for transfers between devices: 732 us -> none  [the longest x1 223 us: device_step(): return add_residual(residual, lax.psum(ffn_part, 'tp'))]
    pallas_call x0 -> x12, Pallas kernels: none -> 407 us  [the longest x4 140 us: attention(): pl.pallas_call(functools.partial(attention_body, heads, block, head_dim,...]
    ppermute x0 -> x18, waiting for transfers between devices: none -> 322 us  [the longest x12 190 us: device_step(): lax.ppermute(w, 'tp', (up, back)[n % 2])]
    all_to_all x1 -> x0, blocking collectives: 279 us -> none  [moe_branch(): received = lax.all_to_all(send, 'ep', 0, 1, tiled=True)]
    dot_general x15 -> x4, matrix products: 269 us -> 23.4 us  [the longest x1 12.7 us: dot(): return jnp.dot(a, b, preferred_element_type=F32)]
    all_to_all x1 -> x4, waiting for transfers between devices: 263 us -> 30.6 us  [the longest x2 30.6 us: device_step(): lax.all_to_all(y, 'ep', 0, 0, tiled=True).reshape(ep * capacity, width)]
    gather x3 -> x0, local copies, waits for them, and re-layouts: 176 us -> none  [the longest x1 79.3 us: dispatch(): return jnp.take(h_flat, slot_token, axis=0, mode='fill', fill_value=0)]
  transfers between devices with their start and end apart: 5 -> 34, of which waited for: 5 -> 15; matrix products, arithmetic and copies ran while one was open for 5% -> 6% of each run, Pallas kernels for 0% -> 31%
where the time goes in v1:
time: 1050 us; the launch traced here: 1040 us
  waiting for transfers between devices  493 us (47%)
  Pallas kernels  407 us (39%)
  local copies, waits for them, and re-layouts  42.1 us (4%)
  starting transfers between devices  39.6 us (4%)
  matrix products  23.4 us (2%)
  between operations  14.5 us (1%)
  blocking collectives  12.3 us (1%)
  other arithmetic  12.1 us (1%)
    ppermute x12, waiting for transfers between devices, device_step(): lax.ppermute(w, 'tp', (up, back)[n % 2])  190 us
    pallas_call x4, Pallas kernels, attention(): pl.pallas_call(functools.partial(attention_body, heads, block, head_dim,...  140 us
    pallas_call x2, Pallas kernels, expert(): pl.pallas_call(expert_body, grid_spec=pltpu.PrefetchScalarGridSpec(num_sc...  88.5 us
    ppermute x3, waiting for transfers between devices, device_step(): from_ahead = [lax.ppermute(w, 'tp', back) for w in near[1]]  78.7 us
    pallas_call x2, Pallas kernels, combine(): pl.pallas_call(combine_body, grid=(tokens // block,), out_shape=jax.Shape...  78.5 us
    all_gather x2, waiting for transfers between devices, device_step(): outs.append(lax.all_gather(out, 'tp', axis=0, tiled=True))  62.9 us
    pallas_call x2, Pallas kernels, dense(): pl.pallas_call(dense_body, grid=(length // step,), out_shape=jax.ShapeDty...  58.7 us
    ppermute x3, waiting for transfers between devices, device_step(): from_behind = [lax.ppermute(w, 'tp', up) for w in near[0]]  53.6 us
  transfers between devices with their start and end apart: 34, of which 15 were waited for; matrix products, arithmetic and copies ran while one was open for 6% of the time, Pallas kernels for 31%

profile of v1, /device:TPU:97, one launch (start us, length us, event | category | flops | bytes accessed | tf_op | source)
XLA Modules:
  0.0 1043.9 jit_solution(16835831889644865737)
XLA Ops:
  6.6 1.6 constant_dynamic-slice_fusion.16
  8.3 1.2 constant_dynamic-slice_fusion.6
  10.5 12.3 %all_gather.44 = f32[2,12,1024]{2,0,1:T(2,128)S(1)} all-gather(f32[2,3,1024]{2,0,1:T(2,128)} %param.17), channel_id=1, replica_groups=mesh['part'=1,'tp'=4,'ep'=8] {'tp'}, dimensions={1}, use_global_device_ids=true | all-gather | bytes 122880 | tf_op jit(solution)/shard_map/all_gather | solution.py:367
  23.9 3.3 constant_dynamic-slice_fusion.7
  27.3 4.0 constant_dynamic-slice_fusion.8
  31.3 1.5 constant_dynamic-slice_fusion.9
  32.8 2.7 constant_dynamic-slice_fusion.12
  35.5 2.0 copy-done.5
  37.5 2.7 constant_dynamic-slice_fusion.10
  40.2 2.1 slice-done.2
  42.4 2.5 constant_dynamic-slice_fusion.11
  44.9 3.9 dynamic-slice_bitcast_fusion
  50.0 2.5 all-gather.16.cloned.1.call-done
  52.5 42.9 %all-gather.14.cloned.1.call-done = bf16[32,3,96,192]{3,2,1,0:T(8,128)(2,1)} async-done(((bf16[1,3,96,192]{3,2,1,0:T(8,128)(2,1)}), bf16[32,3,96,192]{3,2,1,0:T(8,128)(2,1)}) %all-gather.14.cloned.1.call-update) | async-done | bytes 3538960 | tf_op jit(solution)/shard_map/all_gather | solution.py:353
  95.5 34.6 %attention.5 = (bf16[1024,768]{1,0:T(8,128)(2,1)}, bf16[1024,768]{1,0:T(8,128)(2,1)}) custom-call(bf16[1024,768]{1,0:T(8,128)(2,1)} %get-tuple-element.87.refs_0_, f32[1,768]{1,0:T(1,128)} %get-tuple-element.133.refs_1_, f32[1,768]{1,0:T(1,128)} %get-tuple-element.132.refs_2_, bf16[4,8,3,96,192]{4,3,2,1,0:T(8,128)(2,1)} %bitcast.102, ...), custom_call_target="tpu_custom_call" | custom-call | flops 14495514624 | bytes 20000000 | tf_op jit(solution)/shard_map/attention/pallas_call | solution.py:97
  130.6 34.6 %attention.4 = (bf16[1024,768]{1,0:T(8,128)(2,1)}, bf16[1024,768]{1,0:T(8,128)(2,1)}) custom-call(bf16[1024,768]{1,0:T(8,128)(2,1)} %get-tuple-element.88.refs_0_, f32[1,768]{1,0:T(1,128)} %get-tuple-element.133.refs_1_, f32[1,768]{1,0:T(1,128)} %get-tuple-element.132.refs_2_, bf16[4,8,3,96,192]{4,3,2,1,0:T(8,128)(2,1)} %bitcast.103, ...), custom_call_target="tpu_custom_call" | custom-call | flops 14495514624 | bytes 20000000 | tf_op jit(solution)/shard_map/attention/pallas_call | solution.py:97
  167.2 1.6 constant_dynamic-slice_fusion.4
  170.2 1.6 collective-permute-start.2
  171.9 1.0 collective-permute-start.3
  172.9 1.2 collective-permute-start.4
  174.1 1.6 constant_dynamic-slice_fusion.3
  176.2 1.2 fusion.11
  177.4 1.1 fusion.5
  178.6 2.0 copy-done.2
  182.7 3.0 add_reduce_fusion
  185.7 31.7 %collective-permute-done = bf16[1,768,768]{2,1,0:T(8,128)(2,1)} collective-permute-done((bf16[1,768,768]{2,1,0:T(8,128)(2,1)}, bf16[1,768,768]{2,1,0:T(8,128)(2,1)}, u32[]{:S(2)}, u32[]{:S(2)}) %collective-permute-start) | collective-permute-done | bytes 1179680 | tf_op jit(solution)/shard_map/ppermute | solution.py:380
  218.0 2.4 select_reduce_fusion
  221.8 12.7 %fusion.10 = s32[32,256]{1,0:T(8,128)S(1)} fusion(s32[16384]{0:T(1024)S(1)} %bitcast.89, bf16[16,16384]{1,0:T(8,128)(2,1)S(1)} %copy-done.10, bf16[16,16384]{1,0:T(8,128)(2,1)S(1)} %copy-done.9), kind=kOutput, calls=%fused_computation.18 | convolution fusion | flops 274735104 | bytes 1146880 | tf_op jit(solution)/shard_map/dot_general | solution.py:19
  234.5 24.8 %collective-permute-done.1 = bf16[1,768,768]{2,1,0:T(8,128)(2,1)} collective-permute-done((bf16[1,768,768]{2,1,0:T(8,128)(2,1)}, bf16[1,768,768]{2,1,0:T(8,128)(2,1)}, u32[]{:S(2)}, u32[]{:S(2)}) %collective-permute-start.1) | collective-permute-done | bytes 1179680 | tf_op jit(solution)/shard_map/ppermute | solution.py:380
  260.5 49.4 %collective-permute-done.2 = bf16[1,768,768]{2,1,0:T(8,128)(2,1)} collective-permute-done((bf16[1,768,768]{2,1,0:T(8,128)(2,1)}, bf16[1,768,768]{2,1,0:T(8,128)(2,1)}, u32[]{:S(2)}, u32[]{:S(2)}) %collective-permute-start.2) | collective-permute-done | bytes 1179680 | tf_op jit(solution)/shard_map/ppermute | solution.py:380
  310.4 1.0 collective-permute-start.6
  311.5 15.4 %all-gather.18.cloned.1.call-done.refs_0_ = bf16[4096,768]{1,0:T(8,128)(2,1)} async-done(((bf16[1024,768]{1,0:T(8,128)(2,1)}), bf16[4096,768]{1,0:T(8,128)(2,1)}) %all-gather.18.cloned.1.call-update) | async-done | bytes 6291472 | tf_op jit(solution)/shard_map/all_gather | solution.py:391
  326.9 29.6 %pick.1 = (bf16[2048,768]{1,0:T(8,128)(2,1)}, bf16[2048,768]{1,0:T(8,128)(2,1)}) custom-call(s32[4096]{0:T(1024)} %bitcast.92, bf16[4096,768]{1,0:T(8,128)(2,1)} %all-gather.18.cloned.1.call-done.refs_0_, bf16[4096,768]{1,0:T(8,128)(2,1)} %all-gather.20.cloned.1.call-done.refs_1_), custom_call_target="tpu_custom_call" | custom-call | flops 20000000000 | bytes 20000000 | tf_op jit(solution)/shard_map/pick/pallas_call | solution.py:250
  356.5 5.1 all-to-all-start.2
  361.6 1.2 collective-permute-start.8
  362.8 17.5 %collective-permute-done.10.refs_7_ = bf16[2,768,768]{2,1,0:T(8,128)(2,1)} collective-permute-done((bf16[2,768,768]{2,1,0:T(8,128)(2,1)}, bf16[2,768,768]{2,1,0:T(8,128)(2,1)}, u32[]{:S(2)}, u32[]{:S(2)}) %collective-permute-start.10) | collective-permute-done | bytes 2359328 | tf_op jit(solution)/shard_map/ppermute | solution.py:382
  380.3 1.3 collective-permute-start.9
  381.6 61.1 %collective-permute-done.11.refs_8_ = bf16[2,768,768]{2,1,0:T(8,128)(2,1)} collective-permute-done((bf16[2,768,768]{2,1,0:T(8,128)(2,1)}, bf16[2,768,768]{2,1,0:T(8,128)(2,1)}, u32[]{:S(2)}, u32[]{:S(2)}) %collective-permute-start.11) | collective-permute-done | bytes 2359328 | tf_op jit(solution)/shard_map/ppermute | solution.py:382
  442.8 1.3 collective-permute-start.15
  444.0 1.5 collective-permute-start.16
  446.1 6.6 all-to-all-start
  452.6 53.6 %collective-permute-done.8.refs_5_ = bf16[2,768,768]{2,1,0:T(8,128)(2,1)} collective-permute-done((bf16[2,768,768]{2,1,0:T(8,128)(2,1)}, bf16[2,768,768]{2,1,0:T(8,128)(2,1)}, u32[]{:S(2)}, u32[]{:S(2)}) %collective-permute-start.8) | collective-permute-done | bytes 2359328 | tf_op jit(solution)/shard_map/ppermute | solution.py:381
  507.2 35.1 %collective-permute-done.15.refs_9_ = bf16[1,768,768]{2,1,0:T(8,128)(2,1)} collective-permute-done((bf16[1,768,768]{2,1,0:T(8,128)(2,1)}, bf16[1,768,768]{2,1,0:T(8,128)(2,1)}, u32[]{:S(2)}, u32[]{:S(2)}) %collective-permute-start.15) | collective-permute-done | bytes 1179680 | tf_op jit(solution)/shard_map/ppermute | solution.py:393
  542.3 1.6 collective-permute-start.14
  543.9 23.7 %collective-permute-done.16.refs_10_ = bf16[1,768,768]{2,1,0:T(8,128)(2,1)} collective-permute-done((bf16[1,768,768]{2,1,0:T(8,128)(2,1)}, bf16[1,768,768]{2,1,0:T(8,128)(2,1)}, u32[]{:S(2)}, u32[]{:S(2)}) %collective-permute-start.16) | collective-permute-done | bytes 1179680 | tf_op jit(solution)/shard_map/ppermute | solution.py:393
  567.6 25.3 %collective-permute-done.17.refs_11_ = bf16[1,768,768]{2,1,0:T(8,128)(2,1)} collective-permute-done((bf16[1,768,768]{2,1,0:T(8,128)(2,1)}, bf16[1,768,768]{2,1,0:T(8,128)(2,1)}, u32[]{:S(2)}, u32[]{:S(2)}) %collective-permute-start.17) | collective-permute-done | bytes 1179680 | tf_op jit(solution)/shard_map/ppermute | solution.py:393
  592.9 44.3 %expert.3 = bf16[8,256,768]{2,1,0:T(8,128)(2,1)} custom-call(s32[1]{0:T(128)} %bitcast.8.me_ref, bf16[8,256,768]{2,1,0:T(8,128)(2,1)} %all-to-all-done.2.rows_ref, bf16[8,768,768]{2,1,0:T(8,128)(2,1)} %refs_0_.3, bf16[8,768,768]{2,1,0:T(8,128)(2,1)} %refs_1_.3, bf16[8,768,768]{2,1,0:T(8,128)(2,1)} %refs_2_.3, ...), custom_call_target="tpu_custom_call" | custom-call | flops 28991029248 | bytes 20000000 | tf_op jit(solution)/shard_map/expert/pallas_call | solution.py:143
  637.1 5.3 all-to-all-start.3
  642.5 0.9 copy-done.20
  643.9 1.1 copy-done.22
  644.9 44.2 %expert.2 = bf16[8,256,768]{2,1,0:T(8,128)(2,1)} custom-call(s32[1]{0:T(128)} %bitcast.8.me_ref, bf16[8,256,768]{2,1,0:T(8,128)(2,1)} %all-to-all-done.rows_ref, bf16[8,768,768]{2,1,0:T(8,128)(2,1)} %refs_0_.3, bf16[8,768,768]{2,1,0:T(8,128)(2,1)} %refs_1_.3, bf16[8,768,768]{2,1,0:T(8,128)(2,1)} %refs_2_.3, ...), custom_call_target="tpu_custom_call" | custom-call | flops 28991029248 | bytes 20000000 | tf_op jit(solution)/shard_map/expert/pallas_call | solution.py:143
  689.2 5.0 all-to-all-start.1
  695.1 4.8 fusion.72
  701.2 30.6 %all-to-all-done.1 = bf16[8,256,768]{2,1,0:T(8,128)(2,1)} async-done(((bf16[8,256,768]{2,1,0:T(8,128)(2,1)}), bf16[8,256,768]{2,1,0:T(8,128)(2,1)}, u32[]{:S(2)}, u32[]{:S(2)}) %all-to-all-start.1) | async-done | bytes 3145760 | tf_op jit(solution)/shard_map/all_to_all | solution.py:424
  731.8 39.0 %combine.3 = bf16[4096,768]{1,0:T(8,128)(2,1)} custom-call(s32[4096]{0:T(1024)} %get-tuple-element.113.r1, s32[4096]{0:T(1024)} %get-tuple-element.140.r2, f32[4096]{0:T(1024)} %get-tuple-element.110.g1, f32[4096]{0:T(1024)} %get-tuple-element.109.g2, bf16[2048,768]{1,0:T(8,128)(2,1)} %bitcast.16.y0, bf16[2048,768]{1,0:T(8,128)(2,1)} %bitcast.18.y1), custom_call_target="tpu_custom_call" | custom-call | flops 20000000000 | bytes 20000000 | tf_op jit(solution)/shard_map/combine/pallas_call | solution.py:320
  770.9 4.8 fusion.71
  776.9 39.5 %combine.2 = bf16[4096,768]{1,0:T(8,128)(2,1)} custom-call(s32[4096]{0:T(1024)} %get-tuple-element.112.r1, s32[4096]{0:T(1024)} %get-tuple-element.141.r2, f32[4096]{0:T(1024)} %get-tuple-element.130.g1, f32[4096]{0:T(1024)} %get-tuple-element.129.g2, bf16[2048,768]{1,0:T(8,128)(2,1)} %bitcast.16.y0, bf16[2048,768]{1,0:T(8,128)(2,1)} %bitcast.18.y1), custom_call_target="tpu_custom_call" | custom-call | flops 20000000000 | bytes 20000000 | tf_op jit(solution)/shard_map/combine/pallas_call | solution.py:320
  816.7 15.2 %reduce-scatter.5.cloned.1.call-done.refs_1_ = bf16[1024,768]{1,0:T(8,128)(2,1)} async-done(((bf16[4096,768]{1,0:T(8,128)(2,1)}), bf16[1024,768]{1,0:T(8,128)(2,1)}) %reduce-scatter.5.cloned.1.call-update) | async-done | bytes 1572880 | tf_op jit(solution)/shard_map/reduce_scatter | solution.py:429
  831.9 35.4 %attention.7 = (bf16[1024,768]{1,0:T(8,128)(2,1)}, bf16[1024,768]{1,0:T(8,128)(2,1)}) custom-call(bf16[1024,768]{1,0:T(8,128)(2,1)} %get-tuple-element.78.refs_0_, bf16[1024,768]{1,0:T(8,128)(2,1)} %reduce-scatter.5.cloned.1.call-done.refs_1_, f32[1,768]{1,0:T(1,128)} %get-tuple-element.134.refs_2_, f32[1,768]{1,0:T(1,128)} %get-tuple-element.131.refs_3_, ...), custom_call_target="tpu_custom_call" | custom-call | flops 14495514624 | bytes 20000000 | tf_op jit(solution)/shard_map/attention/pallas_call | solution.py:97
  867.3 29.4 %dense.3 = bf16[1024,768]{1,0:T(8,128)(2,1)} custom-call(bf16[1024,768]{1,0:T(8,128)(2,1)} %get-tuple-element.79.u_ref, bf16[1024,768]{1,0:T(8,128)(2,1)} %get-tuple-element.80.res_ref, bf16[4,768,768]{2,1,0:T(8,128)(2,1)} %bitcast.96, bf16[4,768,768]{2,1,0:T(8,128)(2,1)} %bitcast.98, bf16[4,768,768]{2,1,0:T(8,128)(2,1)} %bitcast.100), custom_call_target="tpu_custom_call" | custom-call | flops 14495514624 | bytes 18000000 | tf_op jit(solution)/shard_map/dense/pallas_call | solution.py:175
  897.1 35.5 %attention.6 = (bf16[1024,768]{1,0:T(8,128)(2,1)}, bf16[1024,768]{1,0:T(8,128)(2,1)}) custom-call(bf16[1024,768]{1,0:T(8,128)(2,1)} %get-tuple-element.44.refs_0_, bf16[1024,768]{1,0:T(8,128)(2,1)} %reduce-scatter.3.cloned.1.call-done.refs_1_, f32[1,768]{1,0:T(1,128)} %get-tuple-element.134.refs_2_, f32[1,768]{1,0:T(1,128)} %get-tuple-element.131.refs_3_, ...), custom_call_target="tpu_custom_call" | custom-call | flops 14495514624 | bytes 20000000 | tf_op jit(solution)/shard_map/attention/pallas_call | solution.py:97
  932.5 29.3 %dense.2 = bf16[1024,768]{1,0:T(8,128)(2,1)} custom-call(bf16[1024,768]{1,0:T(8,128)(2,1)} %get-tuple-element.73.u_ref, bf16[1024,768]{1,0:T(8,128)(2,1)} %get-tuple-element.74.res_ref, bf16[4,768,768]{2,1,0:T(8,128)(2,1)} %bitcast.97, bf16[4,768,768]{2,1,0:T(8,128)(2,1)} %bitcast.99, bf16[4,768,768]{2,1,0:T(8,128)(2,1)} %bitcast.101), custom_call_target="tpu_custom_call" | custom-call | flops 14495514624 | bytes 18000000 | tf_op jit(solution)/shard_map/dense/pallas_call | solution.py:175
  962.0 62.9 %all-gather.24.cloned.1.call-done.a_ref = bf16[4096,768]{1,0:T(8,128)(2,1)} async-done(((bf16[1024,768]{1,0:T(8,128)(2,1)}), bf16[4096,768]{1,0:T(8,128)(2,1)}) %all-gather.24.cloned.1.call-update) | async-done | bytes 6291472 | tf_op jit(solution)/shard_map/all_gather | solution.py:432
  1024.9 11.9 %join.1 = bf16[8192,768]{1,0:T(8,128)(2,1)} custom-call(bf16[4096,768]{1,0:T(8,128)(2,1)} %all-gather.24.cloned.1.call-done.a_ref, bf16[4096,768]{1,0:T(8,128)(2,1)} %all-gather.26.cloned.1.call-done.b_ref), custom_call_target="tpu_custom_call" | custom-call | flops 5000000000 | bytes 25000000 | tf_op jit(solution)/shard_map/join/pallas_call | solution.py:280
  (148 shorter events, 19.4 us)
Async XLA Ops:
  6.5 159.8 %copy-start = (bf16[768,768]{1,0:T(8,128)(2,1)S(1)}, bf16[768,768]{1,0:T(8,128)(2,1)}, u32[]{:S(2)}) copy-start(bf16[768,768]{1,0:T(8,128)(2,1)} %param.25) | copy-start | bytes 3538948
  6.6 46.0 %all-gather.16.cloned.1.call-start = ((), (), s32[]{:S(2)}) async-start(), calls=%async_computation.7 | async-start | bytes 2433024 | tf_op jit(solution)/shard_map/all_gather | solution.py:353
  8.2 87.2 %all-gather.14.cloned.1.call-start = ((), (), s32[]{:S(2)}) async-start(), calls=%async_computation.6 | async-start | bytes 4866048 | tf_op jit(solution)/shard_map/all_gather | solution.py:353
  10.4 301.1 %all-gather.20.cloned.1.call-start = ((), (), s32[]{:S(2)}) async-start(), calls=%async_computation.9 | async-start | bytes 7864320 | tf_op jit(solution)/shard_map/all_gather | solution.py:391
  23.9 7.4 copy-start.4
  31.3 6.2 copy-start.5
  32.8 7.4 slice-start
  32.8 7.4 slice-start.1
  37.5 4.8 slice-start.2
  44.9 3.9 copy-start.19
  130.1 196.8 %all-gather.18.cloned.1.call-start = ((), (), s32[]{:S(2)}) async-start(), calls=%async_computation.8 | async-start | bytes 7864320 | tf_op jit(solution)/shard_map/all_gather | solution.py:391
  165.3 10.5 %copy-start.17 = (s32[8,1024]{1,0:T(8,128)S(1)}, s32[8,1024]{1,0:T(8,128)}, u32[]{:S(2)}) copy-start(s32[8,1024]{1,0:T(8,128)} %param.16) | copy-start | bytes 98308
  165.3 10.6 %copy-start.18 = (s32[8,1024]{1,0:T(8,128)S(1)}, s32[8,1024]{1,0:T(8,128)}, u32[]{:S(2)}) copy-start(s32[8,1024]{1,0:T(8,128)} %param.15) | copy-start | bytes 98308
  165.3 477.0 %all-gather.22.cloned.1.call-start = ((), (), s32[]{:S(2)}) async-start(), calls=%async_computation.10 | async-start | bytes 4866048 | tf_op jit(solution)/shard_map/all_gather | solution.py:353
  166.3 476.1 %all-gather.28.cloned.1.call-start = ((), (), s32[]{:S(2)}) async-start(), calls=%async_computation.15 | async-start | bytes 4866048 | tf_op jit(solution)/shard_map/all_gather | solution.py:353
  167.1 475.3 %all-gather.30.cloned.1.call-start = ((), (), s32[]{:S(2)}) async-start(), calls=%async_computation.16 | async-start | bytes 4866048 | tf_op jit(solution)/shard_map/all_gather | solution.py:353
  168.8 473.6 %all-gather.32.cloned.1.call-start = ((), (), s32[]{:S(2)}) async-start(), calls=%async_computation.17 | async-start | bytes 4866048 | tf_op jit(solution)/shard_map/all_gather | solution.py:353
  168.9 48.6 %collective-permute-start = (bf16[1,768,768]{2,1,0:T(8,128)(2,1)}, bf16[1,768,768]{2,1,0:T(8,128)(2,1)}, u32[]{:S(2)}, u32[]{:S(2)}) collective-permute-start(bf16[1,768,768]{2,1,0:T(8,128)(2,1)} %get-tuple-element.49), channel_id=1, source_target_pairs={{0,8},{8,16},{16,24},{24,0},{1,9},{9,17},{17,25},{25,1},{2,10},{10... | collective-permute-start | bytes 3538952 | tf_op jit(solution)/shard_map/ppermute | solution.py:380
  169.8 89.5 %collective-permute-start.1 = (bf16[1,768,768]{2,1,0:T(8,128)(2,1)}, bf16[1,768,768]{2,1,0:T(8,128)(2,1)}, u32[]{:S(2)}, u32[]{:S(2)}) collective-permute-start(bf16[1,768,768]{2,1,0:T(8,128)(2,1)} %get-tuple-element.50), channel_id=1, source_target_pairs={{0,8},{8,16},{16,24},{24,0},{1,9},{9,17},{17,25},{25,1},{2,10},{10... | collective-permute-start | bytes 3538952 | tf_op jit(solution)/shard_map/ppermute | solution.py:380
  170.2 139.7 %collective-permute-start.2 = (bf16[1,768,768]{2,1,0:T(8,128)(2,1)}, bf16[1,768,768]{2,1,0:T(8,128)(2,1)}, u32[]{:S(2)}, u32[]{:S(2)}) collective-permute-start(bf16[1,768,768]{2,1,0:T(8,128)(2,1)} %get-tuple-element.51), channel_id=1, source_target_pairs={{0,8},{8,16},{16,24},{24,0},{1,9},{9,17},{17,25},{25,1},{2,10},{10... | collective-permute-start | bytes 3538952 | tf_op jit(solution)/shard_map/ppermute | solution.py:380
  171.9 138.5 %collective-permute-start.3 = (bf16[1,768,768]{2,1,0:T(8,128)(2,1)}, bf16[1,768,768]{2,1,0:T(8,128)(2,1)}, u32[]{:S(2)}, u32[]{:S(2)}) collective-permute-start(bf16[1,768,768]{2,1,0:T(8,128)(2,1)} %get-tuple-element.52), channel_id=1, source_target_pairs={{0,24},{8,0},{16,8},{24,16},{1,25},{9,1},{17,9},{25,17},{2,26},{10... | collective-permute-start | bytes 3538952 | tf_op jit(solution)/shard_map/ppermute | solution.py:380
  172.9 138.5 %collective-permute-start.4 = (bf16[1,768,768]{2,1,0:T(8,128)(2,1)}, bf16[1,768,768]{2,1,0:T(8,128)(2,1)}, u32[]{:S(2)}, u32[]{:S(2)}) collective-permute-start(bf16[1,768,768]{2,1,0:T(8,128)(2,1)} %get-tuple-element.53), channel_id=1, source_target_pairs={{0,24},{8,0},{16,8},{24,16},{1,25},{9,1},{17,9},{25,17},{2,26},{10... | collective-permute-start | bytes 3538952 | tf_op jit(solution)/shard_map/ppermute | solution.py:380
  175.8 2.7 copy-start.11
  175.9 2.7 copy-start.13
  178.5 2.0 copy-start.2
  181.9 35.5 %copy-start.7 = (bf16[1,768,768]{2,1,0:T(8,128)(2,1)S(1)}, bf16[1,768,768]{2,1,0:T(8,128)(2,1)}, u32[]{:S(2)}) copy-start(bf16[1,768,768]{2,1,0:T(8,128)(2,1)} %get-tuple-element.54) | copy-start | bytes 3538948
  182.6 35.4 %copy-start.3 = (f32[32,256,128]{1,2,0:T(8,128)S(1)}, f32[32,256,128]{1,2,0:T(8,128)}, u32[]{:S(2)}) copy-start(f32[32,256,128]{1,2,0:T(8,128)} %copy-done.2) | copy-start | bytes 12582916
  185.7 36.1 %copy-start.9 = (bf16[16,16384]{1,0:T(8,128)(2,1)S(1)}, bf16[16,16384]{1,0:T(8,128)(2,1)}, u32[]{:S(2)}) copy-start(bf16[16,16384]{1,0:T(8,128)(2,1)} %get-tuple-element.107) | copy-start | bytes 1572868
  185.7 36.1 %copy-start.10 = (bf16[16,16384]{1,0:T(8,128)(2,1)S(1)}, bf16[16,16384]{1,0:T(8,128)(2,1)}, u32[]{:S(2)}) copy-start(bf16[16,16384]{1,0:T(8,128)(2,1)} %get-tuple-element.108) | copy-start | bytes 1572868
  217.5 94.0 %collective-permute-start.5 = (bf16[1,768,768]{2,1,0:T(8,128)(2,1)S(1)}, bf16[1,768,768]{2,1,0:T(8,128)(2,1)}, u32[]{:S(2)}, u32[]{:S(2)}) collective-permute-start(bf16[1,768,768]{2,1,0:T(8,128)(2,1)S(1)} %copy-done.7), channel_id=1, source_target_pairs={{0,24},{8,0},{16,8},{24,16},{1,25},{9,1},{17,9},{25,17},{2,26},{10... | collective-permute-start | bytes 3538952 | tf_op jit(solution)/shard_map/ppermute | solution.py:380
  259.3 121.0 %collective-permute-start.10 = (bf16[2,768,768]{2,1,0:T(8,128)(2,1)}, bf16[2,768,768]{2,1,0:T(8,128)(2,1)}, u32[]{:S(2)}, u32[]{:S(2)}) collective-permute-start(bf16[2,768,768]{2,1,0:T(8,128)(2,1)} %get-tuple-element.63), channel_id=1, source_target_pairs={{0,24},{8,0},{16,8},{24,16},{1,25},{9,1},{17,9},{25,17},{2,26},{10... | collective-permute-start | bytes 7077896 | tf_op jit(solution)/shard_map/ppermute | solution.py:382
  309.9 132.9 %collective-permute-start.11 = (bf16[2,768,768]{2,1,0:T(8,128)(2,1)}, bf16[2,768,768]{2,1,0:T(8,128)(2,1)}, u32[]{:S(2)}, u32[]{:S(2)}) collective-permute-start(bf16[2,768,768]{2,1,0:T(8,128)(2,1)} %get-tuple-element.64), channel_id=1, source_target_pairs={{0,24},{8,0},{16,8},{24,16},{1,25},{9,1},{17,9},{25,17},{2,26},{10... | collective-permute-start | bytes 7077896 | tf_op jit(solution)/shard_map/ppermute | solution.py:382
  310.4 133.6 %collective-permute-start.6 = (bf16[2,768,768]{2,1,0:T(8,128)(2,1)}, bf16[2,768,768]{2,1,0:T(8,128)(2,1)}, u32[]{:S(2)}, u32[]{:S(2)}) collective-permute-start(bf16[2,768,768]{2,1,0:T(8,128)(2,1)} %get-tuple-element.59), channel_id=1, source_target_pairs={{0,8},{8,16},{16,24},{24,0},{1,9},{9,17},{17,25},{25,1},{2,10},{10... | collective-permute-start | bytes 7077896 | tf_op jit(solution)/shard_map/ppermute | solution.py:381
  311.4 134.1 %collective-permute-start.7 = (bf16[2,768,768]{2,1,0:T(8,128)(2,1)}, bf16[2,768,768]{2,1,0:T(8,128)(2,1)}, u32[]{:S(2)}, u32[]{:S(2)}) collective-permute-start(bf16[2,768,768]{2,1,0:T(8,128)(2,1)} %get-tuple-element.60), channel_id=1, source_target_pairs={{0,8},{8,16},{16,24},{24,0},{1,9},{9,17},{17,25},{25,1},{2,10},{10... | collective-permute-start | bytes 7077896 | tf_op jit(solution)/shard_map/ppermute | solution.py:381
  356.5 23.9 %copy-start.6 = (bf16[2,768,768]{2,1,0:T(8,128)(2,1)S(1)}, bf16[2,768,768]{2,1,0:T(8,128)(2,1)}, u32[]{:S(2)}) copy-start(bf16[2,768,768]{2,1,0:T(8,128)(2,1)} %get-tuple-element.62) | copy-start | bytes 7077892
  356.5 89.6 %all-to-all-start.2 = ((bf16[8,256,768]{2,1,0:T(8,128)(2,1)}), bf16[8,256,768]{2,1,0:T(8,128)(2,1)}, u32[]{:S(2)}, u32[]{:S(2)}) async-start(bf16[8,256,768]{2,1,0:T(8,128)(2,1)} %bitcast.74), calls=%async_computation.2 | async-start | bytes 6291456 | tf_op jit(solution)/shard_map/all_to_all | solution.py:401
  361.6 144.6 %collective-permute-start.8 = (bf16[2,768,768]{2,1,0:T(8,128)(2,1)}, bf16[2,768,768]{2,1,0:T(8,128)(2,1)}, u32[]{:S(2)}, u32[]{:S(2)}) collective-permute-start(bf16[2,768,768]{2,1,0:T(8,128)(2,1)} %get-tuple-element.61), channel_id=1, source_target_pairs={{0,8},{8,16},{16,24},{24,0},{1,9},{9,17},{17,25},{25,1},{2,10},{10... | collective-permute-start | bytes 7077896 | tf_op jit(solution)/shard_map/ppermute | solution.py:381
  380.3 125.9 %collective-permute-start.9 = (bf16[2,768,768]{2,1,0:T(8,128)(2,1)S(1)}, bf16[2,768,768]{2,1,0:T(8,128)(2,1)}, u32[]{:S(2)}, u32[]{:S(2)}) collective-permute-start(bf16[2,768,768]{2,1,0:T(8,128)(2,1)S(1)} %copy-done.6), channel_id=1, source_target_pairs={{0,24},{8,0},{16,8},{24,16},{1,25},{9,1},{17,9},{25,17},{2,26},{10... | collective-permute-start | bytes 7077896 | tf_op jit(solution)/shard_map/ppermute | solution.py:382
  442.8 99.5 %collective-permute-start.15 = (bf16[1,768,768]{2,1,0:T(8,128)(2,1)}, bf16[1,768,768]{2,1,0:T(8,128)(2,1)}, u32[]{:S(2)}, u32[]{:S(2)}) collective-permute-start(bf16[1,768,768]{2,1,0:T(8,128)(2,1)} %collective-permute-done.3), channel_id=1, source_target_pairs={{0,24},{8,0},{16,8},{24,16},{1,25},{9,1},{17,9},{25,17},{2,26},{10... | collective-permute-start | bytes 3538952 | tf_op jit(solution)/shard_map/ppermute | solution.py:393
  444.0 123.6 %collective-permute-start.16 = (bf16[1,768,768]{2,1,0:T(8,128)(2,1)}, bf16[1,768,768]{2,1,0:T(8,128)(2,1)}, u32[]{:S(2)}, u32[]{:S(2)}) collective-permute-start(bf16[1,768,768]{2,1,0:T(8,128)(2,1)} %collective-permute-done.4), channel_id=1, source_target_pairs={{0,24},{8,0},{16,8},{24,16},{1,25},{9,1},{17,9},{25,17},{2,26},{10... | collective-permute-start | bytes 3538952 | tf_op jit(solution)/shard_map/ppermute | solution.py:393
  445.5 147.3 %collective-permute-start.17 = (bf16[1,768,768]{2,1,0:T(8,128)(2,1)}, bf16[1,768,768]{2,1,0:T(8,128)(2,1)}, u32[]{:S(2)}, u32[]{:S(2)}) collective-permute-start(bf16[1,768,768]{2,1,0:T(8,128)(2,1)} %collective-permute-done.5), channel_id=1, source_target_pairs={{0,24},{8,0},{16,8},{24,16},{1,25},{9,1},{17,9},{25,17},{2,26},{10... | collective-permute-start | bytes 3538952 | tf_op jit(solution)/shard_map/ppermute | solution.py:393
  446.1 191.1 %all-to-all-start = ((bf16[8,256,768]{2,1,0:T(8,128)(2,1)}), bf16[8,256,768]{2,1,0:T(8,128)(2,1)}, u32[]{:S(2)}, u32[]{:S(2)}) async-start(bf16[8,256,768]{2,1,0:T(8,128)(2,1)} %bitcast.73), calls=%async_computation | async-start | bytes 6291456 | tf_op jit(solution)/shard_map/all_to_all | solution.py:401
  506.2 136.2 %collective-permute-start.12 = (bf16[1,768,768]{2,1,0:T(8,128)(2,1)}, bf16[1,768,768]{2,1,0:T(8,128)(2,1)S(1)}, u32[]{:S(2)}, u32[]{:S(2)}) collective-permute-start(bf16[1,768,768]{2,1,0:T(8,128)(2,1)} %collective-permute-done), channel_id=1, source_target_pairs={{0,8},{8,16},{16,24},{24,0},{1,9},{9,17},{17,25},{25,1},{2,10},{10... | collective-permute-start | bytes 3538952 | tf_op jit(solution)/shard_map/ppermute | solution.py:393
  506.2 136.2 %collective-permute-start.13 = (bf16[1,768,768]{2,1,0:T(8,128)(2,1)}, bf16[1,768,768]{2,1,0:T(8,128)(2,1)S(1)}, u32[]{:S(2)}, u32[]{:S(2)}) collective-permute-start(bf16[1,768,768]{2,1,0:T(8,128)(2,1)} %collective-permute-done.1), channel_id=1, source_target_pairs={{0,8},{8,16},{16,24},{24,0},{1,9},{9,17},{17,25},{25,1},{2,10},{10... | collective-permute-start | bytes 3538952 | tf_op jit(solution)/shard_map/ppermute | solution.py:393
  542.3 100.2 %collective-permute-start.14 = (bf16[1,768,768]{2,1,0:T(8,128)(2,1)}, bf16[1,768,768]{2,1,0:T(8,128)(2,1)S(1)}, u32[]{:S(2)}, u32[]{:S(2)}) collective-permute-start(bf16[1,768,768]{2,1,0:T(8,128)(2,1)} %collective-permute-done.2), channel_id=1, source_target_pairs={{0,8},{8,16},{16,24},{24,0},{1,9},{9,17},{17,25},{25,1},{2,10},{10... | collective-permute-start | bytes 3538952 | tf_op jit(solution)/shard_map/ppermute | solution.py:393
  637.1 52.1 %all-to-all-start.3 = ((bf16[8,256,768]{2,1,0:T(8,128)(2,1)}), bf16[8,256,768]{2,1,0:T(8,128)(2,1)}, u32[]{:S(2)}, u32[]{:S(2)}) async-start(bf16[8,256,768]{2,1,0:T(8,128)(2,1)} %expert.3), calls=%async_computation.3 | async-start | bytes 6291456 | tf_op jit(solution)/shard_map/all_to_all | solution.py:424
  642.4 1.0 copy-start.20
  642.5 1.4 copy-start.21
  643.9 1.1 copy-start.22
  689.2 5.1 copy-start.15
  689.2 5.1 copy-start.16
  689.2 5.2 copy-start.12
  689.2 5.2 copy-start.14
  689.2 5.9 copy-start.8
  689.2 42.6 %all-to-all-start.1 = ((bf16[8,256,768]{2,1,0:T(8,128)(2,1)}), bf16[8,256,768]{2,1,0:T(8,128)(2,1)}, u32[]{:S(2)}, u32[]{:S(2)}) async-start(bf16[8,256,768]{2,1,0:T(8,128)(2,1)} %expert.2), calls=%async_computation.1 | async-start | bytes 6291456 | tf_op jit(solution)/shard_map/all_to_all | solution.py:424
  694.2 137.6 %reduce-scatter.5.cloned.1.call-start = ((), (), s32[]{:S(2)}) async-start(), calls=%async_computation.13 | async-start | bytes 7864320 | tf_op jit(solution)/shard_map/reduce_scatter | solution.py:429
  770.8 126.2 %reduce-scatter.3.cloned.1.call-start = ((), (), s32[]{:S(2)}) async-start(), calls=%async_computation.11 | async-start | bytes 7864320 | tf_op jit(solution)/shard_map/reduce_scatter | solution.py:429
  816.5 145.5 %all-gather.26.cloned.1.call-start = ((), (), s32[]{:S(2)}) async-start(), calls=%async_computation.14 | async-start | bytes 7864320 | tf_op jit(solution)/shard_map/all_gather | solution.py:432
  896.7 128.1 %all-gather.24.cloned.1.call-start = ((), (), s32[]{:S(2)}) async-start(), calls=%async_computation.12 | async-start | bytes 7864320 | tf_op jit(solution)/shard_map/all_gather | solution.py:432
  1024.9 12.0 %copy-start.1 = (bf16[768,768]{1,0:T(8,128)(2,1)S(1)}, bf16[768,768]{1,0:T(8,128)(2,1)}, u32[]{:S(2)}) copy-start(bf16[768,768]{1,0:T(8,128)(2,1)} %param.25) | copy-start | bytes 3538948
Sparse Core Ops, SparseCore 0:
  9.4 43.0 all-gather.15
  54.6 40.8 all-gather.13
  130.2 80.3 all-gather.19
  212.1 114.7 all-gather.17
  328.8 54.6 all-gather.21
  385.5 50.8 all-gather.27
  438.5 51.4 all-gather.29
  492.0 50.9 all-gather.31
  771.0 60.8 reduce-scatter.4
  834.1 61.1 reduce-scatter.2
  896.9 62.7 all-gather.25
  962.1 62.7 all-gather.23

commit v2 on v1

v2 whole, which is shorter than its diff:
```python
import functools

import jax
import jax.numpy as jnp
from jax import lax
from jax.experimental import pallas as pl
from jax.experimental.pallas import tpu as pltpu
from jax.sharding import PartitionSpec as P


F32 = jnp.float32
BF16 = jnp.bfloat16
MASKED = -1e30
VMEM_BYTES = 60 << 20
COLS = 256
LANES = 128
TILE = 8


def dot(a, b):
    return jnp.dot(a, b, preferred_element_type=F32)


def norm_rows(wide, gain):
    scale = lax.rsqrt(jnp.mean(wide * wide, axis=-1, keepdims=True) + 1e-6)
    return (wide * scale * gain).astype(BF16)


def whole(*shape):
    return pl.BlockSpec(shape, lambda *_: (0,) * len(shape))


def params():
    return pltpu.CompilerParams(vmem_limit_bytes=VMEM_BYTES)


def cost(flops, nbytes):
    return pl.CostEstimate(flops=int(flops), bytes_accessed=int(nbytes), transcendentals=0)


def attention_body(heads, block, head_dim, layer, has_add, *refs):
    x_ref, refs = refs[0], refs[1:]
    if has_add:
        add_ref, refs = refs[0], refs[1:]
    gain_in, gain_out, qkv_w, out_w, rel_ref, res_ref, u_ref, src_s, acc_s, q_s, k_s, v_s, ctx_s, bias_s = refs
    step = pl.program_id(0)
    length, width = x_ref.shape
    cols = q_s.shape[1]

    @pl.when(step == 0)
    def _():
        wide = x_ref[...].astype(F32)
        if has_add:
            wide = (wide + add_ref[...].astype(F32)).astype(BF16).astype(F32)
        res_ref[...] = wide.astype(BF16)
        src_s[...] = norm_rows(wide, gain_in[...])
        acc_s[...] = jnp.zeros_like(acc_s)

    weight = qkv_w[:, 0].reshape(width, width)
    q_s[...] = dot(src_s[...], weight[:, :cols]).astype(BF16) * jnp.bfloat16(head_dim ** -0.5)
    k_s[...] = dot(src_s[...], weight[:, cols:2 * cols]).astype(BF16)
    v_s[...] = dot(src_s[...], weight[:, 2 * cols:3 * cols]).astype(BF16)
    lane = lax.broadcasted_iota(jnp.int32, (block, cols), 1)
    span = length + block
    terms = rel_ref[:, 0].astype(F32)
    reach = length // terms.shape[0]
    rows = [terms[e, 0:1] + terms[e, 1:2] + terms[e, 2:3] for e in range(terms.shape[0])]
    for head in range(heads):
        at = (layer * heads + head) * reach
        table = jnp.concatenate([row[:, at:at + reach] for row in rows] + [jnp.full((1, block), MASKED, F32)], axis=1)
        spread = jnp.broadcast_to(table, (block, span))
        bias_s[head] = pltpu.roll(spread, span - block + 1, 1, stride=1, stride_axis=0)[:, :length]
    items = [(part, head) for part in range(length // block) for head in range(heads)]

    def scores(part, head):
        keys = (part + 1) * block
        mine = (lane >= head * head_dim) & (lane < (head + 1) * head_dim)
        query = jnp.where(mine, q_s[pl.ds(part * block, block), :], jnp.bfloat16(0))
        logits = lax.dot_general(query, k_s[:keys, :], (((1,), (1,)), ((), ())), preferred_element_type=F32)
        return logits + bias_s[head, :, length - keys:]

    ahead = scores(*items[0])
    context = None
    for n, (part, head) in enumerate(items):
        keys = (part + 1) * block
        logits = ahead
        if n + 1 < len(items):
            ahead = scores(*items[n + 1])
        mine = (lane >= head * head_dim) & (lane < (head + 1) * head_dim)
        grown = jnp.exp(logits - jnp.max(logits, axis=1, keepdims=True))
        weights = (grown * (1.0 / jnp.sum(grown, axis=1, keepdims=True))).astype(BF16)
        out = dot(weights, v_s[:keys, :])
        context = out if head == 0 else jnp.where(mine, out, context)
        if head == heads - 1:
            ctx_s[pl.ds(part * block, block), :] = context.astype(BF16)
    acc_s[...] += dot(ctx_s[:, :heads * head_dim], out_w[:, 0].reshape(heads * head_dim, width))

    @pl.when(step == pl.num_programs(0) - 1)
    def _():
        wide = (res_ref[...].astype(F32) + acc_s[...].astype(BF16).astype(F32)).astype(BF16)
        res_ref[...] = wide
        u_ref[...] = norm_rows(wide.astype(F32), gain_out[...])


def attention(x, add, gain_in, gain_out, layer_w, out_at, first_w, layer, heads, block):
    length, width = x.shape
    peers, parts, first_rows, _ = first_w.shape
    share = width // peers
    head_dim = width // (parts * heads)
    span = heads * head_dim
    cols = -(-span // LANES) * LANES
    out_rows = span // peers
    inputs = [x] if add is None else [x, add]
    flops = 2 * length * width * cols * 4 * parts + 4 * length * length * cols * parts * 3
    return pl.pallas_call(
        functools.partial(attention_body, heads, block, head_dim, layer, add is not None),
        grid=(parts,),
        out_shape=[jax.ShapeDtypeStruct((length, width), BF16)] * 2,
        in_specs=[whole(length, width)] * len(inputs) + [whole(1, width)] * 2 + [
            pl.BlockSpec((peers, 1, share, width), lambda s: (0, s, 0, 0)),
            pl.BlockSpec((peers, 1, out_rows, width), lambda s: (0, s, out_at // out_rows, 0)),
            pl.BlockSpec((peers, 1, TILE, width), lambda s: (0, s, first_rows // TILE - 1, 0))],
        out_specs=[whole(length, width)] * 2,
        scratch_shapes=[pltpu.VMEM((length, width), BF16), pltpu.VMEM((length, width), F32)]
        + [pltpu.VMEM((length, cols), BF16)] * 4 + [pltpu.VMEM((heads, block, length), F32)],
        compiler_params=params(),
        cost_estimate=cost(flops, 20e6),
        name="attention",
    )(*inputs, gain_in[None], gain_out[None], layer_w, layer_w, first_w)


def ffn_quarter(rows, first, second, down, hidden, acc_s, fresh):
    @pl.when(fresh)
    def _():
        acc_s[...] = jnp.zeros_like(acc_s)

    def one(n, carry):
        cut = pl.ds(pl.multiple_of(n * COLS, COLS), COLS)
        act = (jax.nn.gelu(dot(rows, first(cut))) * dot(rows, second(cut))).astype(BF16)
        acc_s[...] += dot(act, down(cut))
        return carry

    lax.fori_loop(0, hidden // COLS, one, 0)


def ffn_body(plan, has_acc, last, me_ref, rows_ref, *refs):
    sources, refs = refs[:len(plan)], refs[len(plan):]
    if has_acc:
        acc_in, refs = refs[0], refs[1:]
    out_ref, weight_s, sems, acc_s = refs
    step = pl.program_id(0)
    rows = rows_ref[...].reshape(-1, rows_ref.shape[-1])
    quarters = weight_s.shape[0]

    def copy(n):
        quarter, matrix, rows, cols, mine = plan[n]
        which = me_ref[0] if mine else 0
        return pltpu.make_async_copy(sources[n].at[which], weight_s.at[quarter, matrix, pl.ds(*rows), pl.ds(*cols)], sems.at[n])

    @pl.when(step == 0)
    def _():
        for n in range(len(plan)):
            copy(n).start()

    if has_acc:
        acc_s[...] = acc_in[...].reshape(acc_s.shape)

    def one(q, carry):
        for n in range(len(plan)):
            @pl.when((step == 0) & (q == plan[n][0]))
            def _():
                copy(n).wait()

        ffn_quarter(rows, lambda cut: weight_s[q, 0, :, cut], lambda cut: weight_s[q, 1, :, cut], lambda cut: weight_s[q, 2, cut, :],
                    weight_s.shape[3], acc_s, (q == 0) & (not has_acc))
        return carry

    lax.fori_loop(0, quarters, one, 0)
    out_ref[...] = (acc_s[...].astype(BF16) if last else acc_s[...]).reshape(out_ref.shape)


def expert(rows, quarters, index, acc, last):
    peers, slots, width = rows.shape
    step = max(1, peers // 2)
    hidden = sum(array.shape[1] for array, _ in quarters[0][2])
    plan, sources = [], []
    for q, quarter in enumerate(quarters):
        for matrix, pieces in enumerate(quarter):
            at, col = 0, 0
            limit = width if matrix == 2 else hidden
            for array, mine in pieces:
                plan.append((q, matrix, (at, array.shape[1]), (col, array.shape[2]), mine))
                sources.append(array)
                col += array.shape[2]
                if col == limit:
                    at, col = at + array.shape[1], 0
    block = pl.BlockSpec((step, slots, width), lambda s, m: (s, 0, 0))
    return pl.pallas_call(
        functools.partial(ffn_body, plan, acc is not None, last),
        grid_spec=pltpu.PrefetchScalarGridSpec(
            num_scalar_prefetch=1,
            grid=(peers // step,),
            in_specs=[block] + [pl.BlockSpec(memory_space=pl.ANY)] * len(sources) + [block] * (acc is not None),
            out_specs=block,
            scratch_shapes=[pltpu.VMEM((len(quarters), 3, width, hidden), BF16), pltpu.SemaphoreType.DMA((len(plan),)),
                            pltpu.VMEM((step * slots, width), F32)]),
        out_shape=jax.ShapeDtypeStruct((peers, slots, width), BF16 if last else F32),
        compiler_params=params(),
        cost_estimate=cost(6 * peers * slots * width * hidden * len(quarters), 20e6),
        name="expert",
    )(index, rows, *sources, *([] if acc is None else [acc]))


def dense_body(u_ref, res_ref, late_ref, out_ref, weight_s, sems, acc_s):
    peers, parts, _, _ = late_ref.shape
    hidden = weight_s.shape[2]
    share = hidden // peers
    rows = u_ref[...]

    def copy(q, matrix, peer):
        return pltpu.make_async_copy(late_ref.at[peer, q, pl.ds((1 + matrix) * share, share)],
                                     weight_s.at[q, matrix, pl.ds(peer * share, share)], sems.at[q])

    def start(q, carry):
        for matrix in range(3):
            for peer in range(peers):
                copy(q, matrix, peer).start()
        return carry

    def one(q, carry):
        for matrix in range(3):
            for peer in range(peers):
                copy(q, matrix, peer).wait()
        ffn_quarter(rows, lambda cut: weight_s[q, 0, :, cut], lambda cut: weight_s[q, 1, :, cut], lambda cut: weight_s[q, 2, cut, :],
                    hidden, acc_s, q == 0)
        return carry

    lax.fori_loop(0, parts, start, 0)
    lax.fori_loop(0, parts, one, 0)
    out_ref[...] = (res_ref[...].astype(F32) + acc_s[...].astype(BF16).astype(F32)).astype(BF16)


def dense(u, res, late_w):
    length, width = u.shape
    peers, parts = late_w.shape[:2]
    share = width // peers
    return pl.pallas_call(
        dense_body,
        out_shape=jax.ShapeDtypeStruct((length, width), BF16),
        in_specs=[pl.BlockSpec(memory_space=pltpu.VMEM)] * 2 + [pl.BlockSpec(memory_space=pl.ANY)],
        out_specs=pl.BlockSpec(memory_space=pltpu.VMEM),
        scratch_shapes=[pltpu.VMEM((parts, 3, peers * share, width), BF16), pltpu.SemaphoreType.DMA((parts,)),
                        pltpu.VMEM((length, width), F32)],
        compiler_params=params(),
        cost_estimate=cost(6 * length * width * width * parts, 18e6),
        name="dense",
    )(u, res, late_w)


def positions(idx_first, idx_second, experts):
    tokens = idx_first.shape[0]
    block = min(256, tokens)
    lane = jnp.arange(2 * experts, dtype=jnp.int32)
    hot = (idx_first[:, None] == lane) | (idx_second[:, None] + experts == lane)
    cells = hot.astype(BF16).reshape(tokens // block, block, 2 * experts)
    lower = jnp.tril(jnp.ones((block, block), BF16))
    within = jnp.einsum("ij,bjn->bin", lower, cells, preferred_element_type=F32)
    totals = within[:, -1, :]
    before = jnp.cumsum(totals, axis=0) - totals
    count = jnp.sum(totals, axis=0)
    shift = jnp.concatenate([jnp.zeros((experts,), F32), count[:experts]]) - 1.0
    ranks = (within + (before + shift)[:, None, :]).reshape(tokens, 2 * experts)
    ranks = jnp.where(hot, ranks, 0.0)
    first = jnp.sum(jnp.where(lane < experts, ranks, 0.0), axis=1)
    second = jnp.sum(jnp.where(lane < experts, 0.0, ranks), axis=1)
    return first.astype(jnp.int32), second.astype(jnp.int32)


def tokens_of_slots(choice, place, owned, capacity):
    number = jnp.arange(1, choice.shape[1] + 1, dtype=jnp.int32)
    number = jnp.concatenate([number, number])
    mine = choice.reshape(-1)[None, :] == owned[:, None]
    high = jnp.where(mine, number // 128, 0).astype(BF16)
    low = jnp.where(mine, number % 128, 0).astype(BF16)
    at_slot = (place.reshape(-1)[:, None] == jnp.arange(capacity, dtype=jnp.int32)).astype(BF16)
    found = dot(jnp.concatenate([high, low]), at_slot).astype(jnp.int32)
    return jnp.maximum(found[: owned.shape[0]] * 128 + found[owned.shape[0]:] - 1, 0)


def to_tiles(tiles, base, ref):
    rows, width = ref.shape

    def sixteen(n, carry):
        r = pl.multiple_of(n * 16, 16)
        for k in range(width // LANES):
            values = ref[pl.ds(r, 16), k * LANES:(k + 1) * LANES].astype(F32)
            for h in range(2):
                tiles[pl.ds((base + r + h * TILE) * TILE + k, TILE, stride=TILE), :] = values[h * TILE:(h + 1) * TILE]
        return carry

    lax.fori_loop(0, rows // 16, sixteen, 0)


def from_tiles(tiles, ref):
    rows, width = ref.shape

    def sixteen(n, carry):
        r = pl.multiple_of(n * 16, 16)
        for k in range(width // LANES):
            values = [tiles[pl.ds((r + h * TILE) * TILE + k, TILE, stride=TILE), :] for h in range(2)]
            ref[pl.ds(r, 16), k * LANES:(k + 1) * LANES] = jnp.concatenate(values).astype(BF16)
        return carry

    lax.fori_loop(0, rows // 16, sixteen, 0)


def tile_at(index):
    return pl.ds(pl.multiple_of(index, TILE), TILE)


def pick_body(half, at_ref, *refs):
    pieces, (out0, out1, tiles, stage) = refs[:-4], refs[-4:]
    step = pl.program_id(0)
    block = out0.shape[0]

    @pl.when(step == 0)
    def _():
        base = 0
        for ref in pieces:
            to_tiles(tiles, base, ref)
            base += ref.shape[0]

    def eight(n, carry):
        for k in range(TILE):
            row = n * TILE + k
            stage[tile_at(row * TILE), :] = tiles[tile_at(at_ref[step * block + row]), :]
        return carry

    lax.fori_loop(0, block // TILE, eight, 0)

    @pl.when(step < half)
    def _():
        from_tiles(stage, out0)

    @pl.when(step >= half)
    def _():
        from_tiles(stage, out1)


def pick(pieces, at):
    count = at.shape[0]
    width = pieces[0].shape[1]
    rows = sum(p.shape[0] for p in pieces)
    block = min(512, count // 2)
    half = count // 2 // block
    return pl.pallas_call(
        functools.partial(pick_body, half),
        grid=(2 * half,),
        out_shape=[jax.ShapeDtypeStruct((count // 2, width), BF16)] * 2,
        in_specs=[pl.BlockSpec(memory_space=pltpu.SMEM)] + [pl.BlockSpec(p.shape, lambda s: (0, 0), pipeline_mode=pl.Buffered(1)) for p in pieces],
        out_specs=[pl.BlockSpec((block, width), lambda s: (jnp.minimum(s, half - 1), 0)),
                   pl.BlockSpec((block, width), lambda s: (jnp.maximum(s - half, 0), 0))],
        scratch_shapes=[pltpu.VMEM((rows * TILE, LANES), F32), pltpu.VMEM((block * TILE, LANES), F32)],
        compiler_params=pltpu.CompilerParams(vmem_limit_bytes=62 << 20),
        cost_estimate=cost(20e9, 20e6),
        name="pick",
    )(at, *pieces)


def combine_body(r1, r2, g1, g2, y0, y1, out_ref, tiles, stage):
    step = pl.program_id(0)
    rows, _ = y0.shape
    block = out_ref.shape[0]

    @pl.when(step == 0)
    def _():
        to_tiles(tiles, 0, y0)
        to_tiles(tiles, rows, y1)
        tiles[pl.ds(2 * rows * TILE, TILE), :] = jnp.zeros((TILE, LANES), F32)

    def eight(n, carry):
        for k in range(TILE):
            row = n * TILE + k
            t = step * block + row
            stage[tile_at(row * TILE), :] = g1[t] * tiles[tile_at(r1[t]), :] + g2[t] * tiles[tile_at(r2[t]), :]
        return carry

    lax.fori_loop(0, block // TILE, eight, 0)
    from_tiles(stage, out_ref)


def combine(rows, gates, y0, y1):
    tokens = rows[0].shape[0]
    width = y0.shape[1]
    block = min(512, tokens)
    smem = pl.BlockSpec(memory_space=pltpu.SMEM)
    return pl.pallas_call(
        combine_body,
        grid=(tokens // block,),
        out_shape=jax.ShapeDtypeStruct((tokens, width), BF16),
        in_specs=[smem] * 4 + [whole(*y0.shape)] * 2,
        out_specs=pl.BlockSpec((block, width), lambda s: (s, 0)),
        scratch_shapes=[pltpu.VMEM(((2 * y0.shape[0] + 1) * TILE, LANES), F32), pltpu.VMEM((block * TILE, LANES), F32)],
        compiler_params=params(),
        cost_estimate=cost(15e9, 20e6),
        name="combine",
    )(*rows, *gates, y0, y1)


def place_body(plan, row_ref, *refs):
    pieces, out_ref, sems = refs[:len(plan)], refs[-2], refs[-1]
    copies = []
    for n, (turn, at) in enumerate(plan):
        row = pl.multiple_of(row_ref[turn] + at, 2 * TILE)
        copies.append(pltpu.make_async_copy(pieces[n], out_ref.at[pl.ds(row, pieces[n].shape[0])], sems.at[n]))
    for copy in copies:
        copy.start()
    for copy in copies:
        copy.wait()


def place(plan, rows, pieces, out):
    fresh = isinstance(out, tuple)
    return pl.pallas_call(
        functools.partial(place_body, plan),
        out_shape=jax.ShapeDtypeStruct(out if fresh else out.shape, BF16),
        in_specs=[pl.BlockSpec(memory_space=pltpu.SMEM)] + [pl.BlockSpec(memory_space=pltpu.VMEM)] * len(pieces)
        + [pl.BlockSpec(memory_space=pl.ANY)] * (not fresh),
        out_specs=pl.BlockSpec(memory_space=pl.ANY),
        scratch_shapes=[pltpu.SemaphoreType.DMA((len(pieces),))],
        input_output_aliases={} if fresh else {1 + len(pieces): 0},
        compiler_params=params(),
        cost_estimate=cost(3e9, 12e6),
        name="place",
    )(rows, *pieces, *([] if fresh else [out]))


def split_terms(wide):
    terms = []
    for _ in range(3):
        term = lax.reduce_precision(wide, exponent_bits=8, mantissa_bits=7)
        terms.append(term.astype(BF16))
        wide = wide - term
    return terms


def pack_qkv(weight, layer, spot, share, cols):
    piece = lax.dynamic_slice(weight, (layer, 0, spot * share, 0), (1, 3, share, weight.shape[3]))[0]
    piece = jnp.pad(piece, ((0, 0), (0, 0), (0, cols - piece.shape[2])))
    return jnp.concatenate([piece[n] for n in range(3)], axis=1)


def pack_out(attn_out, layer, spot, ep):
    rows = attn_out.shape[1] // ep
    return lax.dynamic_slice(attn_out, (layer, spot * rows, 0), (1, rows, attn_out.shape[2]))[0]


def pack_rel(rel_bias, width, spot, ep):
    length = rel_bias.shape[2]
    reach = length // ep
    backward = rel_bias.reshape(-1, length)[:, ::-1]
    terms = split_terms(lax.dynamic_slice_in_dim(backward, spot * reach, reach, 1).reshape(1, width))
    return jnp.concatenate(terms + [jnp.zeros((TILE - 3, width), BF16)])


def solution(mesh):
    row_spec = P(("part", "ep"))
    in_specs = (row_spec, row_spec, row_spec, P(None, "tp"), P(), P(None, None, None, "tp"), P(None, "tp"), P(), P("ep", None, "tp"), P("ep", None, "tp"), P("ep", "tp"), P(None, "tp"), P(None, "tp"), P("tp"))
    tp, ep = mesh.shape["tp"], mesh.shape["ep"]
    up = [(d, (d + 1) % tp) for d in range(tp)]
    back = [(d, (d - 1) % tp) for d in range(tp)]

    def device_step(x_in, idx_first, idx_second, rel_bias, norm_gain, attn_qkv, attn_out, gate_w, expert_w0, expert_w1, expert_down, dense_w0, dense_w1, dense_down):
        num_seqs, length, width = x_in.shape
        experts = gate_w.shape[1]
        tokens = num_seqs * length
        capacity = (2 * tokens + experts - 1) // experts
        me, spot = lax.axis_index("tp"), lax.axis_index("ep")
        chunks = num_seqs // tp
        held = experts // ep
        count = held // tp
        block = min(256, length)
        share = width // ep
        heads = rel_bias.shape[1]
        cols = -(-attn_qkv.shape[3] // LANES) * LANES

        def send_up(w):
            return lax.ppermute(w, "tp", up)

        def send_back(w):
            return lax.ppermute(w, "tp", back)

        def over_tp(piece):
            return lax.all_gather(piece, "tp", axis=0, tiled=False)

        def over_ep(piece):
            return lax.all_gather(piece, "ep", axis=0, tiled=False)

        first = jnp.concatenate([pack_qkv(attn_qkv, 0, spot, share, cols), pack_out(attn_out, 0, spot, ep), pack_rel(rel_bias, width, spot, ep)])
        first_w = over_ep(over_tp(first))
        late = jnp.concatenate([pack_qkv(attn_qkv, 1, spot, share, cols)]
                               + [lax.dynamic_slice_in_dim(w, spot * share, share, 0) for w in (dense_w0, dense_w1, dense_down)]
                               + [pack_out(attn_out, 1, spot, ep)])

        weights = (expert_w0, expert_w1, expert_down)

        def quarter(owner, e):
            return [lax.dynamic_slice_in_dim(w, owner * count + e, 1, 0) for w in weights]

        half = expert_down.shape[1] // 2
        far_up, far_back = [], []
        for e in range(count):
            w0, w1, wd = quarter((me + 2) % tp, e)
            far_up.append([w0, wd[:, :half]])
            far_back.append([w1, wd[:, half:]])

        def halves(w0, w1, wd):
            return [[w0[:, :, cut], w1[:, :, cut], wd[:, cut]] for cut in (slice(0, half), slice(half, 2 * half))]

        near_up = [[quarter((me + 1) % tp, e)] for e in range(count - 1)] + [halves(*quarter((me + 1) % tp, count - 1))]
        near_back = [[quarter((me - 1) % tp, e)] for e in range(count - 1)] + [halves(*quarter((me - 1) % tp, count - 1))]

        x = [lax.dynamic_index_in_dim(x_in, c * tp + me, 0, keepdims=False) for c in range(chunks)]
        far_back[-1][-1], near_up, near_back, x = lax.optimization_barrier((far_back[-1][-1], near_up, near_back, x))

        far_up = [[send_up(w) for w in ws] for ws in far_up]
        far_back = [[send_back(w) for w in ws] for ws in far_back]
        late = over_tp(late)
        late_w = over_ep(late)
        res, own, behind, ahead, across = [], [], [], [], []
        for c in range(chunks):
            r, u = attention(x[c], None, norm_gain[0], norm_gain[1], first_w, share, first_w, 0, heads, block)
            res.append(r)
            own.append(u)
            behind.append(send_up(u))
            ahead.append(send_back(u))

        first_idx, second_idx, _ = lax.optimization_barrier((idx_first.reshape(-1), idx_second.reshape(-1), own[-1]))
        ranks = positions(first_idx, second_idx, experts)
        owned = (jnp.arange(count, dtype=jnp.int32)[:, None] + me * count + jnp.arange(ep, dtype=jnp.int32) * held).reshape(-1)
        token = tokens_of_slots(jnp.stack([first_idx, second_idx]), jnp.stack(ranks), owned, capacity).reshape(-1)
        seq = token // length
        turn = (seq % tp - me) % tp
        turn = jnp.where(turn == tp - 1, 1, jnp.where(turn == 1, 2, jnp.where(turn == 2, 3, 0)))
        at = (((seq // tp) * tp + turn) * length + token % length) * TILE

        mid = length // 2
        for c in range(chunks):
            if c == chunks - 1:
                behind[c], ahead[c], near_up, near_back, at = lax.optimization_barrier((behind[c], ahead[c], near_up, near_back, at))
            across.append([send_up(behind[c][:mid]), send_back(ahead[c][mid:])])
        from_behind, from_ahead, far = [], [], []
        for e in range(count):
            from_behind.append([[send_up(w) for w in ws] for ws in near_up[e]])
            from_ahead.append([[send_back(w) for w in ws] for ws in near_back[e]])
            far.append(([send_up(w) for w in far_up[e]], [send_back(w) for w in far_back[e]]))

        pieces = [p for c in range(chunks) for p in (own[c], behind[c], ahead[c], *across[c])]
        send = pick(pieces, at)
        recv = [lax.all_to_all(send[e].reshape(ep, capacity, width), "ep", 0, 0, tiled=True) for e in range(count)]

        recv[0], pieces = lax.optimization_barrier((recv[0], pieces))

        lane = jnp.arange(experts, dtype=jnp.int32)
        probs = jax.nn.softmax(jnp.dot(jnp.concatenate(pieces), gate_w, preferred_element_type=F32), axis=-1)
        order = jnp.array([0, tp - 1, 1, 2], jnp.int32)
        seqs = (jnp.arange(chunks, dtype=jnp.int32)[:, None] * tp + (order + me) % tp).reshape(-1)
        both = []
        for idx in (idx_first, idx_second):
            turned = jnp.take(idx, seqs, axis=0).reshape(-1)
            both.append(jnp.sum(jnp.where(turned[:, None] == lane, probs, 0.0), axis=1))
        total = both[0] + both[1]
        inverse = jnp.array([0, 2, 3, 1], jnp.int32)
        spots = (jnp.arange(chunks, dtype=jnp.int32)[:, None] * tp + inverse[(jnp.arange(tp) - me) % tp]).reshape(-1)
        gates = [jnp.take((g / total).reshape(num_seqs, length), spots, axis=0).reshape(chunks, -1) for g in both]
        none = count * ep * capacity
        rows = []
        for n, idx in enumerate((first_idx, second_idx)):
            local = idx % held
            mine = (ranks[n] < capacity) & (local // count == me)
            row = (local % count) * (ep * capacity) + idx // held * capacity + ranks[n]
            rows.append((jnp.where(mine, row, none) * TILE).reshape(chunks, -1))

        index = (me * count).astype(jnp.int32)[None]
        returned = []
        for e in range(count):
            mine = [[(w, True)] for w in weights]
            a, b = far[e]
            across_w = [[(a[0], False)], [(b[0], False)], [(a[1], False), (b[1], False)]]
            near = [[[(w, False)] for w in ws] for ws in (from_behind[e][0], from_ahead[e][0])]
            if e:
                recv[e], y = lax.optimization_barrier((recv[e], y))
                returned.append(lax.all_to_all(y, "ep", 0, 0, tiled=True).reshape(ep * capacity, width))
            if e < count - 1:
                partial = expert(recv[e], [mine] + near, index + e, None, False)
                y = expert(recv[e], [across_w], index + e, partial, True)
            else:
                partial = expert(recv[e], [mine, across_w], index + e, None, False)
                for n, (ws, vs) in enumerate(zip(from_behind[e], from_ahead[e])):
                    both_w = [[(w, False), (v, False)] for w, v in zip(ws, vs)]
                    if n and returned:
                        partial, returned[-1] = lax.optimization_barrier((partial, returned[-1]))
                    partial = expert(recv[e], [both_w], index + e, partial, n == len(from_behind[e]) - 1)
                y = partial
        returned.append(lax.all_to_all(y, "ep", 0, 0, tiled=True).reshape(ep * capacity, width))

        order_rows = jnp.stack([(me + turn) % tp for turn in (0, tp - 1, 1, 2)]).astype(jnp.int32) * length
        out = (tokens, width)
        for c in range(chunks):
            part = combine([r[c] for r in rows], [g[c] for g in gates], *returned)
            mixed = lax.psum_scatter(part, "tp", scatter_dimension=0, tiled=True)
            r, u = attention(res[c], mixed, norm_gain[2], norm_gain[3], late_w, 4 * share, first_w, 1, heads, block)
            cuts = 1 if c < chunks - 1 else 2
            size = length // cuts
            plan, pieces = [], []
            for n in range(cuts):
                y = dense(u[n * size:(n + 1) * size], r[n * size:(n + 1) * size], late_w)
                low, high = send_up(y), send_back(y)
                arrived = [y, low, high, send_up(low[:size // 2]), send_back(high[size // 2:])]
                plan += [(turn, n * size + at) for turn, at in ((0, 0), (1, 0), (2, 0), (3, 0), (3, size // 2))]
                pieces += arrived
            out = place(tuple(plan), order_rows + c * tp * length, pieces, out)
        return out.reshape(num_seqs, length, width)

    return jax.shard_map(device_step, mesh=mesh, in_specs=in_specs, out_specs=row_spec, check_vma=False)
```

time: 1050 us -> 987 us (0.940)
  waiting for transfers between devices: 493 us -> 362 us
  starting transfers between devices: 39.6 us -> 95.1 us
  local copies, waits for them, and re-layouts: 42.1 us -> 91.9 us
  Pallas kernels: 407 us -> 361 us
    ppermute x18 -> x54, waiting for transfers between devices: 322 us -> 243 us  [the longest x27 191 us: send_up(): return lax.ppermute(w, 'tp', up)]
    all_gather x10 -> x3, waiting for transfers between devices: 124 us -> 56.9 us  [the longest x2 56.9 us: over_ep(): return lax.all_gather(piece, 'ep', axis=0, tiled=False)]
    ppermute x18 -> x54, starting transfers between devices: 16.2 us -> 61 us  [the longest x27 51.9 us: send_back(): return lax.ppermute(w, 'tp', back)]
    pallas_call x2, Pallas kernels: 78.5 us -> 48 us  [combine(): pl.pallas_call(combine_body, grid=(tokens // block,), out_shape=jax.Shape...]
    unnamed x67 -> x107, local copies, waits for them, and re-layouts: 11 us -> 38 us
    pallas_call x4, Pallas kernels: 140 us -> 115 us  [attention(): pl.pallas_call(functools.partial(attention_body, heads, block, head_dim,...]
    slice x3 -> x17, local copies, waits for them, and re-layouts: 8.86 us -> 29.7 us  [the longest x4 7.48 us: device_step(): across.append([send_up(behind[c][:mid]), send_back(ahead[c][mid:])])]
    reduce_scatter x2, waiting for transfers between devices: 15.2 us -> 35.5 us  [device_step(): mixed = lax.psum_scatter(part, 'tp', scatter_dimension=0, tiled=True)]
  transfers between devices with their start and end apart: 34 -> 63, of which waited for: 15 -> 22; matrix products, arithmetic and copies ran while one was open for 6% -> 12% of each run, Pallas kernels for 31% -> 34%
where the time goes in v2:
time: 987 us; the launch traced here: 977 us
  waiting for transfers between devices  362 us (37%)
  Pallas kernels  361 us (37%)
  starting transfers between devices  95.1 us (10%)
  local copies, waits for them, and re-layouts  91.9 us (9%)
  matrix products  22.3 us (2%)
  between operations  16.2 us (2%)
  blocking collectives  15.2 us (2%)
  other arithmetic  12.8 us (1%)
    ppermute x27, waiting for transfers between devices, send_up(): return lax.ppermute(w, 'tp', up)  191 us
    pallas_call x4, Pallas kernels, attention(): pl.pallas_call(functools.partial(attention_body, heads, block, head_dim,...  115 us
    pallas_call x5, Pallas kernels, expert(): pl.pallas_call(functools.partial(ffn_body, plan, acc is not None, last),...  107 us
    all_gather x2, waiting for transfers between devices, over_ep(): return lax.all_gather(piece, 'ep', axis=0, tiled=False)  56.9 us
    pallas_call x3, Pallas kernels, dense(): pl.pallas_call(dense_body, out_shape=jax.ShapeDtypeStruct((length, width)...  55.7 us
    ppermute x27, waiting for transfers between devices, send_back(): return lax.ppermute(w, 'tp', back)  52.9 us
    ppermute x27, starting transfers between devices, send_back(): return lax.ppermute(w, 'tp', back)  51.9 us
    pallas_call x2, Pallas kernels, combine(): pl.pallas_call(combine_body, grid=(tokens // block,), out_shape=jax.Shape...  48 us
  transfers between devices with their start and end apart: 63, of which 22 were waited for; matrix products, arithmetic and copies ran while one was open for 12% of the time, Pallas kernels for 34%

profile of v2, /device:TPU:97, one launch (start us, length us, event | category | flops | bytes accessed | tf_op | source)
XLA Modules:
  0.0 976.6 jit_solution(4781347976839642535)
XLA Ops:
  11.8 15.2 %all-gather = bf16[512,768]{1,0:T(8,128)(2,1)} all-gather(bf16[128,768]{1,0:T(8,128)(2,1)S(1)} %concatenate.25), channel_id=2, replica_groups=mesh['part'=1,'tp'=4,'ep'=8] {'tp'}, dimensions={0}, use_global_device_ids=true | all-gather | bytes 983040 | tf_op jit(solution)/shard_map/all_gather | solution.py:494
  27.2 3.3 constant_dynamic-slice_fusion.17
  30.4 3.9 constant_dynamic-slice_fusion.18
  35.9 4.7 dynamic-slice_bitcast_fusion
  50.2 19.4 %all-gather.8.cloned.1.call-done = bf16[32,128,768]{2,1,0:T(8,128)(2,1)} async-done(((bf16[4,128,768]{2,1,0:T(8,128)(2,1)}), bf16[32,128,768]{2,1,0:T(8,128)(2,1)}) %all-gather.8.cloned.1.call-update) | async-done | bytes 6291472 | tf_op jit(solution)/shard_map/all_gather | solution.py:497
  69.5 28.2 %attention.4 = (bf16[1024,768]{1,0:T(8,128)(2,1)}, bf16[1024,768]{1,0:T(8,128)(2,1)}) custom-call(bf16[1024,768]{1,0:T(8,128)(2,1)} %get-tuple-element.76.refs_0_, f32[1,768]{1,0:T(1,128)} %get-tuple-element.213.refs_1_, f32[1,768]{1,0:T(1,128)} %get-tuple-element.212.refs_2_, bf16[8,4,128,768]{3,2,1,0:T(8,128)(2,1)} %bitcast.160, ...), custom_call_target="tpu_custom_call" | custom-call | flops 19327352832 | bytes 20000000 | tf_op jit(solution)/shard_map/attention/pallas_call | solution.py:115
  100.9 28.2 %attention.5 = (bf16[1024,768]{1,0:T(8,128)(2,1)}, bf16[1024,768]{1,0:T(8,128)(2,1)}) custom-call(bf16[1024,768]{1,0:T(8,128)(2,1)} %get-tuple-element.100.refs_0_, f32[1,768]{1,0:T(1,128)} %get-tuple-element.213.refs_1_, f32[1,768]{1,0:T(1,128)} %get-tuple-element.212.refs_2_, bf16[8,4,128,768]{3,2,1,0:T(8,128)(2,1)} %bitcast.163, ...), custom_call_target="tpu_custom_call" | custom-call | flops 19327352832 | bytes 20000000 | tf_op jit(solution)/shard_map/attention/pallas_call | solution.py:115
  129.1 2.8 collective-permute-start.3
  136.5 3.1 add_reduce_fusion
  142.4 12.7 %fusion.12 = s32[32,256]{1,0:T(8,128)S(1)} fusion(s32[16384]{0:T(1024)S(1)} %bitcast.146, bf16[16,16384]{1,0:T(8,128)(2,1)S(1)} %get-tuple-element.194, bf16[16,16384]{1,0:T(8,128)(2,1)S(1)} %get-tuple-element.193), kind=kOutput, calls=%fused_computation.30 | convolution fusion | flops 274735104 | bytes 1146880 | tf_op jit(solution)/shard_map/dot_general | solution.py:21
  159.2 2.7 collective-permute-start.7
  161.9 6.8 collective-permute-done.2.refs_1_
  172.9 2.7 collective-permute-start.5
  176.4 9.0 collective-permute-done.6.refs_8_
  185.6 2.7 collective-permute-start.14
  188.3 14.1 %collective-permute-done.4.refs_3_ = bf16[512,768]{1,0:T(8,128)(2,1)} collective-permute-done((bf16[512,768]{1,0:T(8,128)(2,1)}, bf16[512,768]{1,0:T(8,128)(2,1)}, u32[]{:S(2)}, u32[]{:S(2)}) %collective-permute-start.4) | collective-permute-done | bytes 786464 | tf_op jit(solution)/shard_map/ppermute | solution.py:488
  203.9 24.4 %pick.1 = (bf16[2048,768]{1,0:T(8,128)(2,1)}, bf16[2048,768]{1,0:T(8,128)(2,1)}) custom-call(s32[4096]{0:T(1024)} %fusion.56.at_ref, bf16[1024,768]{1,0:T(8,128)(2,1)} %get-tuple-element.105.refs_0_, bf16[1024,768]{1,0:T(8,128)(2,1)} %collective-permute-done.2.refs_1_, bf16[1024,768]{1,0:T(8,128)(2,1)} %collective-permute-done.3.refs_2_, ...), custom_call_target="tpu_custom_call" | custom-call | flops 20000000000 | bytes 20000000 | tf_op jit(solution)/shard_map/pick/pallas_call | solution.py:356
  228.3 6.2 all-to-all-start
  243.1 10.0 %collective-permute-done.34 = bf16[1,384,768]{2,1,0:T(8,128)(2,1)} collective-permute-done((bf16[1,384,768]{2,1,0:T(8,128)(2,1)}, bf16[1,384,768]{2,1,0:T(8,128)(2,1)}, u32[]{:S(2)}, u32[]{:S(2)}) %collective-permute-start.34) | collective-permute-done | bytes 589856 | tf_op jit(solution)/shard_map/ppermute | solution.py:491
  253.1 2.7 collective-permute-start.30
  261.6 7.9 collective-permute-done.8
  269.6 83.3 %collective-permute-done.13.refs_2_ = bf16[1,384,768]{2,1,0:T(8,128)(2,1)} collective-permute-done((bf16[1,384,768]{2,1,0:T(8,128)(2,1)}, bf16[1,384,768]{2,1,0:T(8,128)(2,1)}, u32[]{:S(2)}, u32[]{:S(2)}) %collective-permute-start.13) | collective-permute-done | bytes 589856 | tf_op jit(solution)/shard_map/ppermute | solution.py:488
  352.9 2.7 collective-permute-start.19
  360.1 7.6 all-to-all-start.1
  368.3 9.9 %collective-permute-done.17.refs_4_ = bf16[1,768,768]{2,1,0:T(8,128)(2,1)} collective-permute-done((bf16[1,768,768]{2,1,0:T(8,128)(2,1)}, bf16[1,768,768]{2,1,0:T(8,128)(2,1)}, u32[]{:S(2)}, u32[]{:S(2)}) %collective-permute-start.17) | collective-permute-done | bytes 1179680 | tf_op jit(solution)/shard_map/ppermute | solution.py:488
  379.2 24.2 %collective-permute-done.18.refs_5_ = bf16[1,768,768]{2,1,0:T(8,128)(2,1)} collective-permute-done((bf16[1,768,768]{2,1,0:T(8,128)(2,1)}, bf16[1,768,768]{2,1,0:T(8,128)(2,1)}, u32[]{:S(2)}, u32[]{:S(2)}) %collective-permute-start.18) | collective-permute-done | bytes 1179680 | tf_op jit(solution)/shard_map/ppermute | solution.py:488
  405.0 24.5 %collective-permute-done.21.refs_8_ = bf16[1,768,768]{2,1,0:T(8,128)(2,1)} collective-permute-done((bf16[1,768,768]{2,1,0:T(8,128)(2,1)}, bf16[1,768,768]{2,1,0:T(8,128)(2,1)}, u32[]{:S(2)}, u32[]{:S(2)}) %collective-permute-start.21) | collective-permute-done | bytes 1179680 | tf_op jit(solution)/shard_map/ppermute | solution.py:491
  429.5 3.6 collective-permute-start.31
  433.2 34.0 %expert.5.refs_4_ = f32[8,256,768]{2,1,0:T(8,128)} custom-call(s32[1]{0:T(128)} %bitcast.19.me_ref, bf16[8,256,768]{2,1,0:T(8,128)(2,1)} %copy-done.9, bf16[8,768,768]{2,1,0:T(8,128)(2,1)} %refs_0_.3, bf16[8,768,768]{2,1,0:T(8,128)(2,1)} %refs_1_.3, bf16[8,768,768]{2,1,0:T(8,128)(2,1)} %refs_2_.3, bf16[1,768,768]{2,1,0:T(8,128)(2,1)} %collective-permute-done.16.refs_3_, ...), custom_call_target="tpu_custom_call" | custom-call | flops 21743271936 | bytes 20000000 | tf_op jit(solution)/shard_map/expert/pallas_call | solution.py:198
  469.7 15.9 %expert.6 = bf16[8,256,768]{2,1,0:T(8,128)(2,1)} custom-call(s32[1]{0:T(128)} %bitcast.19.me_ref, bf16[8,256,768]{2,1,0:T(8,128)(2,1)} %copy-done.9, bf16[1,768,768]{2,1,0:T(8,128)(2,1)} %copy-done.30, bf16[1,768,768]{2,1,0:T(8,128)(2,1)} %copy-done.29, bf16[1,384,768]{2,1,0:T(8,128)(2,1)} %collective-permute-done.13.refs_2_, ...), custom_call_target="tpu_custom_call" | custom-call | flops 7247757312 | bytes 20000000 | tf_op jit(solution)/shard_map/expert/pallas_call | solution.py:198
  485.7 11.2 %all-to-all-start.2 = ((bf16[8,256,768]{2,1,0:T(8,128)(2,1)}), bf16[8,256,768]{2,1,0:T(8,128)(2,1)S(1)}, u32[]{:S(2)}, u32[]{:S(2)}) async-start(bf16[8,256,768]{2,1,0:T(8,128)(2,1)} %expert.6), calls=%async_computation.2 | async-start | bytes 6291456 | tf_op jit(solution)/shard_map/all_to_all | solution.py:593
  496.9 8.5 collective-permute-done.35.refs_6_
  505.4 3.4 collective-permute-start.23
  508.8 2.7 collective-permute-start.25
  511.5 24.6 %expert.7.refs_6_ = f32[8,256,768]{2,1,0:T(8,128)} custom-call(s32[1]{0:T(128)S(6)} %add.407.me_ref, bf16[8,256,768]{2,1,0:T(8,128)(2,1)} %all-to-all-done.1.rows_ref, bf16[8,768,768]{2,1,0:T(8,128)(2,1)} %refs_0_.3, bf16[8,768,768]{2,1,0:T(8,128)(2,1)} %refs_1_.3, bf16[8,768,768]{2,1,0:T(8,128)(2,1)} %refs_2_.3, ...), custom_call_target="tpu_custom_call" | custom-call | flops 14495514624 | bytes 20000000 | tf_op jit(solution)/shard_map/expert/pallas_call | solution.py:198
  536.1 2.7 constant_dynamic-update-slice_fusion.9
  538.8 2.7 constant_dynamic-update-slice_fusion.8
  541.4 2.7 constant_dynamic-update-slice_fusion.7
  548.4 2.7 collective-permute-start.27
  555.0 2.8 constant_dynamic-update-slice_fusion.2
  559.6 2.7 collective-permute-start.37
  562.3 2.7 collective-permute-start.39
  568.9 16.6 %expert.8.refs_6_ = f32[8,256,768]{2,1,0:T(8,128)} custom-call(s32[1]{0:T(128)S(6)} %add.407.me_ref, bf16[8,256,768]{2,1,0:T(8,128)(2,1)} %all-to-all-done.1.rows_ref, bf16[1,768,384]{2,1,0:T(8,128)(2,1)} %collective-permute-done.22.refs_0_, bf16[1,768,384]{2,1,0:T(8,128)(2,1)} %collective-permute-done.23.refs_1_, ...), custom_call_target="tpu_custom_call" | custom-call | flops 7247757312 | bytes 20000000 | tf_op jit(solution)/shard_map/expert/pallas_call | solution.py:198
  585.5 3.1 collective-permute-done.40.refs_4_
  588.7 9.5 collective-permute-done.41.refs_5_
  598.2 16.0 %expert.9 = bf16[8,256,768]{2,1,0:T(8,128)(2,1)} custom-call(s32[1]{0:T(128)S(6)} %add.407.me_ref, bf16[8,256,768]{2,1,0:T(8,128)(2,1)} %all-to-all-done.1.rows_ref, bf16[1,768,384]{2,1,0:T(8,128)(2,1)} %copy-done.31, bf16[1,768,384]{2,1,0:T(8,128)(2,1)} %collective-permute-done.37.refs_1_, bf16[1,768,384]{2,1,0:T(8,128)(2,1)} %collective-permute-done.38.refs_2_, ...), custom_call_target="tpu_custom_call" | custom-call | flops 7247757312 | bytes 20000000 | tf_op jit(solution)/shard_map/expert/pallas_call | solution.py:198
  614.2 8.8 all-to-all-start.3
  623.0 8.5 fusion.79
  635.2 25.2 %all-to-all-done.3 = bf16[8,256,768]{2,1,0:T(8,128)(2,1)S(1)} async-done(((bf16[8,256,768]{2,1,0:T(8,128)(2,1)}), bf16[8,256,768]{2,1,0:T(8,128)(2,1)S(1)}, u32[]{:S(2)}, u32[]{:S(2)}) %all-to-all-start.3) | async-done | bytes 3145760 | tf_op jit(solution)/shard_map/all_to_all | solution.py:605
  662.1 24.0 %combine.3 = bf16[4096,768]{1,0:T(8,128)(2,1)} custom-call(s32[4096]{0:T(1024)} %get-tuple-element.203.r1, s32[4096]{0:T(1024)} %get-tuple-element.201.r2, f32[4096]{0:T(1024)} %bitcast.150, f32[4096]{0:T(1024)} %bitcast.148, bf16[2048,768]{1,0:T(8,128)(2,1)} %bitcast.122, bf16[2048,768]{1,0:T(8,128)(2,1)} %bitcast.125), custom_call_target="tpu_custom_call" | custom-call | flops 15000000512 | bytes 20000000 | tf_op jit(solution)/shard_map/combine/pallas_call | solution.py:397
  688.5 24.0 %combine.2 = bf16[4096,768]{1,0:T(8,128)(2,1)} custom-call(s32[4096]{0:T(1024)} %get-tuple-element.204.r1, s32[4096]{0:T(1024)} %get-tuple-element.202.r2, f32[4096]{0:T(1024)} %bitcast.151, f32[4096]{0:T(1024)} %bitcast.149, bf16[2048,768]{1,0:T(8,128)(2,1)} %bitcast.123, bf16[2048,768]{1,0:T(8,128)(2,1)} %bitcast.126), custom_call_target="tpu_custom_call" | custom-call | flops 15000000512 | bytes 20000000 | tf_op jit(solution)/shard_map/combine/pallas_call | solution.py:397
  712.5 35.5 %reduce-scatter.5.cloned.1.call-done.refs_1_ = bf16[1024,768]{1,0:T(8,128)(2,1)} async-done(((bf16[4096,768]{1,0:T(8,128)(2,1)}), bf16[1024,768]{1,0:T(8,128)(2,1)}) %reduce-scatter.5.cloned.1.call-update) | async-done | bytes 1572880 | tf_op jit(solution)/shard_map/reduce_scatter | solution.py:611
  748.0 37.6 %all-gather.12.cloned.1.call-done = bf16[32,408,768]{2,1,0:T(8,128)(2,1)} async-done(((bf16[4,408,768]{2,1,0:T(8,128)(2,1)}), bf16[32,408,768]{2,1,0:T(8,128)(2,1)}) %all-gather.12.cloned.1.call-update) | async-done | bytes 20054032 | tf_op jit(solution)/shard_map/all_gather | solution.py:497
  785.6 29.3 %attention.7 = (bf16[1024,768]{1,0:T(8,128)(2,1)}, bf16[1024,768]{1,0:T(8,128)(2,1)}) custom-call(bf16[1024,768]{1,0:T(8,128)(2,1)} %get-tuple-element.142.refs_0_, bf16[1024,768]{1,0:T(8,128)(2,1)} %reduce-scatter.5.cloned.1.call-done.refs_1_, f32[1,768]{1,0:T(1,128)} %get-tuple-element.214.refs_2_, f32[1,768]{1,0:T(1,128)} %get-tuple-element.211.refs_3_, ...), custom_call_target="tpu_custom_call" | custom-call | flops 19327352832 | bytes 20000000 | tf_op jit(solution)/shard_map/attention/pallas_call | solution.py:115
  814.8 24.4 %dense.5.refs_0_ = bf16[1024,768]{1,0:T(8,128)(2,1)} custom-call(bf16[1024,768]{1,0:T(8,128)(2,1)} %get-tuple-element.143.u_ref, bf16[1024,768]{1,0:T(8,128)(2,1)} %get-tuple-element.144.res_ref, bf16[8,4,408,768]{3,2,1,0:T(8,128)(2,1)} %bitcast.155), custom_call_target="tpu_custom_call" | custom-call | flops 14495514624 | bytes 18000000 | tf_op jit(solution)/shard_map/dense/pallas_call | solution.py:247
  842.2 29.0 %attention.6 = (bf16[1024,768]{1,0:T(8,128)(2,1)}, bf16[1024,768]{1,0:T(8,128)(2,1)}) custom-call(bf16[1024,768]{1,0:T(8,128)(2,1)} %get-tuple-element.77.refs_0_, bf16[1024,768]{1,0:T(8,128)(2,1)} %reduce-scatter.3.cloned.1.call-done.refs_1_, f32[1,768]{1,0:T(1,128)} %get-tuple-element.214.refs_2_, f32[1,768]{1,0:T(1,128)} %get-tuple-element.211.refs_3_, ...), custom_call_target="tpu_custom_call" | custom-call | flops 19327352832 | bytes 20000000 | tf_op jit(solution)/shard_map/attention/pallas_call | solution.py:115
  871.2 2.8 fusion.74
  875.2 15.7 %dense.4.refs_5_ = bf16[512,768]{1,0:T(8,128)(2,1)} custom-call(bf16[512,768]{1,0:T(8,128)(2,1)} %get-tuple-element.185.u_ref, bf16[512,768]{1,0:T(8,128)(2,1)} %get-tuple-element.183.res_ref, bf16[8,4,408,768]{3,2,1,0:T(8,128)(2,1)} %bitcast.158), custom_call_target="tpu_custom_call" | custom-call | flops 7247757312 | bytes 18000000 | tf_op jit(solution)/shard_map/dense/pallas_call | solution.py:247
  893.7 15.7 %dense.3.refs_0_ = bf16[512,768]{1,0:T(8,128)(2,1)} custom-call(bf16[512,768]{1,0:T(8,128)(2,1)} %get-tuple-element.186.u_ref, bf16[512,768]{1,0:T(8,128)(2,1)} %get-tuple-element.184.res_ref, bf16[8,4,408,768]{3,2,1,0:T(8,128)(2,1)} %bitcast.159), custom_call_target="tpu_custom_call" | custom-call | flops 7247757312 | bytes 18000000 | tf_op jit(solution)/shard_map/dense/pallas_call | solution.py:247
  920.3 8.4 collective-permute-done.42.refs_1_
  932.3 13.2 %collective-permute-done.52.refs_3_ = bf16[512,768]{1,0:T(8,128)(2,1)} collective-permute-done((bf16[512,768]{1,0:T(8,128)(2,1)}, bf16[512,768]{1,0:T(8,128)(2,1)}, u32[]{:S(2)}, u32[]{:S(2)}) %collective-permute-start.52) | collective-permute-done | bytes 786464 | tf_op jit(solution)/shard_map/ppermute | solution.py:488
  946.2 5.5 place.2.refs_10_
  953.9 8.4 collective-permute-done.44.refs_3_
  963.2 5.6 place.3
  (282 shorter events, 108.4 us)
Async XLA Ops:
  7.4 615.5 %copy-start = (f32[768,64]{0,1:T(8,128)S(1)}, f32[768,64]{0,1:T(8,128)}, u32[]{:S(2)}) copy-start(f32[768,64]{0,1:T(8,128)} %param.27) | copy-start | bytes 589828
  7.4 62.1 %all-gather.8.cloned.1.call-start = ((), (), s32[]{:S(2)}) async-start(), calls=%async_computation.8 | async-start | bytes 7077888 | tf_op jit(solution)/shard_map/all_gather | solution.py:497
  97.8 58.1 %collective-permute-start = (bf16[1024,768]{1,0:T(8,128)(2,1)}, bf16[1024,768]{1,0:T(8,128)(2,1)}, u32[]{:S(2)}, u32[]{:S(2)}) collective-permute-start(bf16[1024,768]{1,0:T(8,128)(2,1)} %get-tuple-element.110.refs_5_), channel_id=1, source_target_pairs={{0,8},{8,16},{16,24},{24,0},{1,9},{9,17},{17,25},{25,1},{2,10},{10... | collective-permute-start | bytes 4718600 | tf_op jit(solution)/shard_map/ppermute | solution.py:488
  99.0 56.9 %collective-permute-start.1 = (bf16[1024,768]{1,0:T(8,128)(2,1)}, bf16[1024,768]{1,0:T(8,128)(2,1)}, u32[]{:S(2)}, u32[]{:S(2)}) collective-permute-start(bf16[1024,768]{1,0:T(8,128)(2,1)} %get-tuple-element.110.refs_5_), channel_id=1, source_target_pairs={{0,24},{8,0},{16,8},{24,16},{1,25},{9,1},{17,9},{25,17},{2,26},{10... | collective-permute-start | bytes 4718600 | tf_op jit(solution)/shard_map/ppermute | solution.py:491
  129.1 39.6 %collective-permute-start.2 = (bf16[1024,768]{1,0:T(8,128)(2,1)}, bf16[1024,768]{1,0:T(8,128)(2,1)}, u32[]{:S(2)}, u32[]{:S(2)}) collective-permute-start(bf16[1024,768]{1,0:T(8,128)(2,1)} %get-tuple-element.105.refs_0_), channel_id=1, source_target_pairs={{0,8},{8,16},{16,24},{24,0},{1,9},{9,17},{17,25},{25,1},{2,10},{10... | collective-permute-start | bytes 4718600 | tf_op jit(solution)/shard_map/ppermute | solution.py:488
  129.1 41.7 %collective-permute-start.3 = (bf16[1024,768]{1,0:T(8,128)(2,1)}, bf16[1024,768]{1,0:T(8,128)(2,1)}, u32[]{:S(2)}, u32[]{:S(2)}) collective-permute-start(bf16[1024,768]{1,0:T(8,128)(2,1)} %get-tuple-element.105.refs_0_), channel_id=1, source_target_pairs={{0,24},{8,0},{16,8},{24,16},{1,25},{9,1},{17,9},{25,17},{2,26},{10... | collective-permute-start | bytes 4718600 | tf_op jit(solution)/shard_map/ppermute | solution.py:491
  157.9 27.5 %collective-permute-start.6 = (bf16[512,768]{1,0:T(8,128)(2,1)}, bf16[512,768]{1,0:T(8,128)(2,1)S(1)}, u32[]{:S(2)}, u32[]{:S(2)}) collective-permute-start(bf16[512,768]{1,0:T(8,128)(2,1)} %slice.194), channel_id=1, source_target_pairs={{0,8},{8,16},{16,24},{24,0},{1,9},{9,17},{17,25},{25,1},{2,10},{10... | collective-permute-start | bytes 2359304 | tf_op jit(solution)/shard_map/ppermute | solution.py:488
  159.2 26.4 %collective-permute-start.7 = (bf16[512,768]{1,0:T(8,128)(2,1)S(1)}, bf16[512,768]{1,0:T(8,128)(2,1)S(1)}, u32[]{:S(2)}, u32[]{:S(2)}) collective-permute-start(bf16[512,768]{1,0:T(8,128)(2,1)S(1)} %slice.195), channel_id=1, source_target_pairs={{0,24},{8,0},{16,8},{24,16},{1,25},{9,1},{17,9},{25,17},{2,26},{10... | collective-permute-start | bytes 2359304 | tf_op jit(solution)/shard_map/ppermute | solution.py:491
  170.7 31.6 %collective-permute-start.4 = (bf16[512,768]{1,0:T(8,128)(2,1)}, bf16[512,768]{1,0:T(8,128)(2,1)}, u32[]{:S(2)}, u32[]{:S(2)}) collective-permute-start(bf16[512,768]{1,0:T(8,128)(2,1)} %slice.235), channel_id=1, source_target_pairs={{0,8},{8,16},{16,24},{24,0},{1,9},{9,17},{17,25},{25,1},{2,10},{10... | collective-permute-start | bytes 2359304 | tf_op jit(solution)/shard_map/ppermute | solution.py:488
  172.9 30.8 %collective-permute-start.5 = (bf16[512,768]{1,0:T(8,128)(2,1)}, bf16[512,768]{1,0:T(8,128)(2,1)}, u32[]{:S(2)}, u32[]{:S(2)}) collective-permute-start(bf16[512,768]{1,0:T(8,128)(2,1)} %slice.236), channel_id=1, source_target_pairs={{0,24},{8,0},{16,8},{24,16},{1,25},{9,1},{17,9},{25,17},{2,26},{10... | collective-permute-start | bytes 2359304 | tf_op jit(solution)/shard_map/ppermute | solution.py:491
  175.5 81.8 %collective-permute-start.10 = (bf16[1,768,768]{2,1,0:T(8,128)(2,1)}, bf16[1,768,768]{2,1,0:T(8,128)(2,1)}, u32[]{:S(2)}, u32[]{:S(2)}) collective-permute-start(bf16[1,768,768]{2,1,0:T(8,128)(2,1)} %get-tuple-element.162), channel_id=1, source_target_pairs={{0,24},{8,0},{16,8},{24,16},{1,25},{9,1},{17,9},{25,17},{2,26},{10... | collective-permute-start | bytes 3538952 | tf_op jit(solution)/shard_map/ppermute | solution.py:491
  185.4 55.4 %collective-permute-start.12 = (bf16[1,384,768]{2,1,0:T(8,128)(2,1)}, bf16[1,384,768]{2,1,0:T(8,128)(2,1)}, u32[]{:S(2)}, u32[]{:S(2)}) collective-permute-start(bf16[1,384,768]{2,1,0:T(8,128)(2,1)} %get-tuple-element.154), channel_id=1, source_target_pairs={{0,8},{8,16},{16,24},{24,0},{1,9},{9,17},{17,25},{25,1},{2,10},{10... | collective-permute-start | bytes 1769480 | tf_op jit(solution)/shard_map/ppermute | solution.py:488
  185.6 56.1 %collective-permute-start.14 = (bf16[1,384,768]{2,1,0:T(8,128)(2,1)}, bf16[1,384,768]{2,1,0:T(8,128)(2,1)}, u32[]{:S(2)}, u32[]{:S(2)}) collective-permute-start(bf16[1,384,768]{2,1,0:T(8,128)(2,1)} %get-tuple-element.158), channel_id=1, source_target_pairs={{0,24},{8,0},{16,8},{24,16},{1,25},{9,1},{17,9},{25,17},{2,26},{10... | collective-permute-start | bytes 1769480 | tf_op jit(solution)/shard_map/ppermute | solution.py:491
  202.4 50.7 %collective-permute-start.34 = (bf16[1,384,768]{2,1,0:T(8,128)(2,1)}, bf16[1,384,768]{2,1,0:T(8,128)(2,1)}, u32[]{:S(2)}, u32[]{:S(2)}) collective-permute-start(bf16[1,384,768]{2,1,0:T(8,128)(2,1)} %get-tuple-element.130), channel_id=1, source_target_pairs={{0,24},{8,0},{16,8},{24,16},{1,25},{9,1},{17,9},{25,17},{2,26},{10... | collective-permute-start | bytes 1769480 | tf_op jit(solution)/shard_map/ppermute | solution.py:491
  203.7 52.1 %collective-permute-start.32 = (bf16[1,384,768]{2,1,0:T(8,128)(2,1)}, bf16[1,384,768]{2,1,0:T(8,128)(2,1)}, u32[]{:S(2)}, u32[]{:S(2)}) collective-permute-start(bf16[1,384,768]{2,1,0:T(8,128)(2,1)} %get-tuple-element.153), channel_id=1, source_target_pairs={{0,8},{8,16},{16,24},{24,0},{1,9},{9,17},{17,25},{25,1},{2,10},{10... | collective-permute-start | bytes 1769480 | tf_op jit(solution)/shard_map/ppermute | solution.py:488
  228.3 130.1 %all-to-all-start = ((bf16[8,256,768]{2,1,0:T(8,128)(2,1)}), bf16[8,256,768]{2,1,0:T(8,128)(2,1)S(1)}, u32[]{:S(2)}, u32[]{:S(2)}) async-start(bf16[8,256,768]{2,1,0:T(8,128)(2,1)} %bitcast.124), calls=%async_computation | async-start | bytes 6291456 | tf_op jit(solution)/shard_map/all_to_all | solution.py:560
  234.5 451.8 %all-gather.10.cloned.1.call-start = ((), (), s32[]{:S(2)}) async-start(), calls=%async_computation.9 | async-start | bytes 3133440 | tf_op jit(solution)/shard_map/all_gather | solution.py:494
  240.8 28.7 %collective-permute-start.8 = (bf16[1,768,768]{2,1,0:T(8,128)(2,1)}, bf16[1,768,768]{2,1,0:T(8,128)(2,1)}, u32[]{:S(2)}, u32[]{:S(2)}) collective-permute-start(bf16[1,768,768]{2,1,0:T(8,128)(2,1)} %get-tuple-element.166), channel_id=1, source_target_pairs={{0,8},{8,16},{16,24},{24,0},{1,9},{9,17},{17,25},{25,1},{2,10},{10... | collective-permute-start | bytes 3538952 | tf_op jit(solution)/shard_map/ppermute | solution.py:488
  241.7 111.2 %collective-permute-start.28 = (bf16[1,768,768]{2,1,0:T(8,128)(2,1)}, bf16[1,768,768]{2,1,0:T(8,128)(2,1)}, u32[]{:S(2)}, u32[]{:S(2)}) collective-permute-start(bf16[1,768,768]{2,1,0:T(8,128)(2,1)} %get-tuple-element.165), channel_id=1, source_target_pairs={{0,8},{8,16},{16,24},{24,0},{1,9},{9,17},{17,25},{25,1},{2,10},{10... | collective-permute-start | bytes 3538952 | tf_op jit(solution)/shard_map/ppermute | solution.py:488
  253.1 102.5 %collective-permute-start.30 = (bf16[1,768,768]{2,1,0:T(8,128)(2,1)}, bf16[1,768,768]{2,1,0:T(8,128)(2,1)}, u32[]{:S(2)}, u32[]{:S(2)}) collective-permute-start(bf16[1,768,768]{2,1,0:T(8,128)(2,1)} %get-tuple-element.161), channel_id=1, source_target_pairs={{0,24},{8,0},{16,8},{24,16},{1,25},{9,1},{17,9},{25,17},{2,26},{10... | collective-permute-start | bytes 3538952 | tf_op jit(solution)/shard_map/ppermute | solution.py:491
  255.8 99.9 %collective-permute-start.16 = (bf16[1,768,768]{2,1,0:T(8,128)(2,1)}, bf16[1,768,768]{2,1,0:T(8,128)(2,1)}, u32[]{:S(2)}, u32[]{:S(2)}) collective-permute-start(bf16[1,768,768]{2,1,0:T(8,128)(2,1)} %get-tuple-element.117), channel_id=1, source_target_pairs={{0,8},{8,16},{16,24},{24,0},{1,9},{9,17},{17,25},{25,1},{2,10},{10... | collective-permute-start | bytes 3538952 | tf_op jit(solution)/shard_map/ppermute | solution.py:488
  257.3 95.6 %collective-permute-start.13 = (bf16[1,384,768]{2,1,0:T(8,128)(2,1)}, bf16[1,384,768]{2,1,0:T(8,128)(2,1)}, u32[]{:S(2)}, u32[]{:S(2)}) collective-permute-start(bf16[1,384,768]{2,1,0:T(8,128)(2,1)} %collective-permute-done.12), channel_id=1, source_target_pairs={{0,8},{8,16},{16,24},{24,0},{1,9},{9,17},{17,25},{25,1},{2,10},{10... | collective-permute-start | bytes 1769480 | tf_op jit(solution)/shard_map/ppermute | solution.py:488
  269.5 108.6 %collective-permute-start.17 = (bf16[1,768,768]{2,1,0:T(8,128)(2,1)}, bf16[1,768,768]{2,1,0:T(8,128)(2,1)}, u32[]{:S(2)}, u32[]{:S(2)}) collective-permute-start(bf16[1,768,768]{2,1,0:T(8,128)(2,1)} %get-tuple-element.118), channel_id=1, source_target_pairs={{0,8},{8,16},{16,24},{24,0},{1,9},{9,17},{17,25},{25,1},{2,10},{10... | collective-permute-start | bytes 3538952 | tf_op jit(solution)/shard_map/ppermute | solution.py:488
  352.9 50.6 %collective-permute-start.18 = (bf16[1,768,768]{2,1,0:T(8,128)(2,1)}, bf16[1,768,768]{2,1,0:T(8,128)(2,1)}, u32[]{:S(2)}, u32[]{:S(2)}) collective-permute-start(bf16[1,768,768]{2,1,0:T(8,128)(2,1)} %get-tuple-element.119), channel_id=1, source_target_pairs={{0,8},{8,16},{16,24},{24,0},{1,9},{9,17},{17,25},{25,1},{2,10},{10... | collective-permute-start | bytes 3538952 | tf_op jit(solution)/shard_map/ppermute | solution.py:488
  352.9 51.6 %collective-permute-start.19 = (bf16[1,768,768]{2,1,0:T(8,128)(2,1)}, bf16[1,768,768]{2,1,0:T(8,128)(2,1)}, u32[]{:S(2)}, u32[]{:S(2)}) collective-permute-start(bf16[1,768,768]{2,1,0:T(8,128)(2,1)} %get-tuple-element.120), channel_id=1, source_target_pairs={{0,24},{8,0},{16,8},{24,16},{1,25},{9,1},{17,9},{25,17},{2,26},{10... | collective-permute-start | bytes 3538952 | tf_op jit(solution)/shard_map/ppermute | solution.py:491
  355.6 49.3 %collective-permute-start.20 = (bf16[1,768,768]{2,1,0:T(8,128)(2,1)}, bf16[1,768,768]{2,1,0:T(8,128)(2,1)}, u32[]{:S(2)}, u32[]{:S(2)}) collective-permute-start(bf16[1,768,768]{2,1,0:T(8,128)(2,1)} %get-tuple-element.121), channel_id=1, source_target_pairs={{0,24},{8,0},{16,8},{24,16},{1,25},{9,1},{17,9},{25,17},{2,26},{10... | collective-permute-start | bytes 3538952 | tf_op jit(solution)/shard_map/ppermute | solution.py:491
  355.7 73.9 %collective-permute-start.21 = (bf16[1,768,768]{2,1,0:T(8,128)(2,1)}, bf16[1,768,768]{2,1,0:T(8,128)(2,1)}, u32[]{:S(2)}, u32[]{:S(2)}) collective-permute-start(bf16[1,768,768]{2,1,0:T(8,128)(2,1)} %get-tuple-element.122), channel_id=1, source_target_pairs={{0,24},{8,0},{16,8},{24,16},{1,25},{9,1},{17,9},{25,17},{2,26},{10... | collective-permute-start | bytes 3538952 | tf_op jit(solution)/shard_map/ppermute | solution.py:491
  360.1 125.6 %all-to-all-start.1 = ((bf16[8,256,768]{2,1,0:T(8,128)(2,1)}), bf16[8,256,768]{2,1,0:T(8,128)(2,1)}, u32[]{:S(2)}, u32[]{:S(2)}) async-start(bf16[8,256,768]{2,1,0:T(8,128)(2,1)} %bitcast.20), calls=%async_computation.1 | async-start | bytes 6291456 | tf_op jit(solution)/shard_map/all_to_all | solution.py:560
  378.2 89.0 %collective-permute-start.15 = (bf16[1,384,768]{2,1,0:T(8,128)(2,1)}, bf16[1,384,768]{2,1,0:T(8,128)(2,1)S(1)}, u32[]{:S(2)}, u32[]{:S(2)}) collective-permute-start(bf16[1,384,768]{2,1,0:T(8,128)(2,1)} %collective-permute-done.14), channel_id=1, source_target_pairs={{0,24},{8,0},{16,8},{24,16},{1,25},{9,1},{17,9},{25,17},{2,26},{10... | collective-permute-start | bytes 1769480 | tf_op jit(solution)/shard_map/ppermute | solution.py:491
  403.4 64.0 %collective-permute-start.11 = (bf16[1,768,768]{2,1,0:T(8,128)(2,1)}, bf16[1,768,768]{2,1,0:T(8,128)(2,1)S(1)}, u32[]{:S(2)}, u32[]{:S(2)}) collective-permute-start(bf16[1,768,768]{2,1,0:T(8,128)(2,1)} %collective-permute-done.10), channel_id=1, source_target_pairs={{0,24},{8,0},{16,8},{24,16},{1,25},{9,1},{17,9},{25,17},{2,26},{10... | collective-permute-start | bytes 3538952 | tf_op jit(solution)/shard_map/ppermute | solution.py:491
  404.5 64.2 %collective-permute-start.9 = (bf16[1,768,768]{2,1,0:T(8,128)(2,1)}, bf16[1,768,768]{2,1,0:T(8,128)(2,1)S(1)}, u32[]{:S(2)}, u32[]{:S(2)}) collective-permute-start(bf16[1,768,768]{2,1,0:T(8,128)(2,1)} %collective-permute-done.8), channel_id=1, source_target_pairs={{0,8},{8,16},{16,24},{24,0},{1,9},{9,17},{17,25},{25,1},{2,10},{10... | collective-permute-start | bytes 3538952 | tf_op jit(solution)/shard_map/ppermute | solution.py:488
  404.9 103.9 %collective-permute-start.29 = (bf16[1,768,768]{2,1,0:T(8,128)(2,1)}, bf16[1,768,768]{2,1,0:T(8,128)(2,1)}, u32[]{:S(2)}, u32[]{:S(2)}) collective-permute-start(bf16[1,768,768]{2,1,0:T(8,128)(2,1)} %collective-permute-done.28), channel_id=1, source_target_pairs={{0,8},{8,16},{16,24},{24,0},{1,9},{9,17},{17,25},{25,1},{2,10},{10... | collective-permute-start | bytes 3538952 | tf_op jit(solution)/shard_map/ppermute | solution.py:488
  429.5 81.9 %collective-permute-start.31 = (bf16[1,768,768]{2,1,0:T(8,128)(2,1)}, bf16[1,768,768]{2,1,0:T(8,128)(2,1)}, u32[]{:S(2)}, u32[]{:S(2)}) collective-permute-start(bf16[1,768,768]{2,1,0:T(8,128)(2,1)} %collective-permute-done.30), channel_id=1, source_target_pairs={{0,24},{8,0},{16,8},{24,16},{1,25},{9,1},{17,9},{25,17},{2,26},{10... | collective-permute-start | bytes 3538952 | tf_op jit(solution)/shard_map/ppermute | solution.py:491
  467.2 38.2 %collective-permute-start.35 = (bf16[1,384,768]{2,1,0:T(8,128)(2,1)}, bf16[1,384,768]{2,1,0:T(8,128)(2,1)}, u32[]{:S(2)}, u32[]{:S(2)}) collective-permute-start(bf16[1,384,768]{2,1,0:T(8,128)(2,1)} %collective-permute-done.34), channel_id=1, source_target_pairs={{0,24},{8,0},{16,8},{24,16},{1,25},{9,1},{17,9},{25,17},{2,26},{10... | collective-permute-start | bytes 1769480 | tf_op jit(solution)/shard_map/ppermute | solution.py:491
  467.5 41.3 %collective-permute-start.33 = (bf16[1,384,768]{2,1,0:T(8,128)(2,1)}, bf16[1,384,768]{2,1,0:T(8,128)(2,1)}, u32[]{:S(2)}, u32[]{:S(2)}) collective-permute-start(bf16[1,384,768]{2,1,0:T(8,128)(2,1)} %collective-permute-done.32), channel_id=1, source_target_pairs={{0,8},{8,16},{16,24},{24,0},{1,9},{9,17},{17,25},{25,1},{2,10},{10... | collective-permute-start | bytes 1769480 | tf_op jit(solution)/shard_map/ppermute | solution.py:488
  468.7 79.6 %collective-permute-start.22 = (bf16[1,768,384]{2,1,0:T(8,128)(2,1)}, bf16[1,768,384]{2,1,0:T(8,128)(2,1)}, u32[]{:S(2)}, u32[]{:S(2)}) collective-permute-start(bf16[1,768,384]{2,1,0:T(8,128)(2,1)} %get-tuple-element.124), channel_id=1, source_target_pairs={{0,8},{8,16},{16,24},{24,0},{1,9},{9,17},{17,25},{25,1},{2,10},{10... | collective-permute-start | bytes 1769480 | tf_op jit(solution)/shard_map/ppermute | solution.py:488
  485.7 99.8 %all-to-all-start.2 = ((bf16[8,256,768]{2,1,0:T(8,128)(2,1)}), bf16[8,256,768]{2,1,0:T(8,128)(2,1)S(1)}, u32[]{:S(2)}, u32[]{:S(2)}) async-start(bf16[8,256,768]{2,1,0:T(8,128)(2,1)} %expert.6), calls=%async_computation.2 | async-start | bytes 6291456 | tf_op jit(solution)/shard_map/all_to_all | solution.py:593
  505.4 45.7 %collective-permute-start.23 = (bf16[1,768,384]{2,1,0:T(8,128)(2,1)}, bf16[1,768,384]{2,1,0:T(8,128)(2,1)}, u32[]{:S(2)}, u32[]{:S(2)}) collective-permute-start(bf16[1,768,384]{2,1,0:T(8,128)(2,1)} %get-tuple-element.125), channel_id=1, source_target_pairs={{0,24},{8,0},{16,8},{24,16},{1,25},{9,1},{17,9},{25,17},{2,26},{10... | collective-permute-start | bytes 1769480 | tf_op jit(solution)/shard_map/ppermute | solution.py:491
  508.8 50.8 %collective-permute-start.24 = (bf16[1,768,384]{2,1,0:T(8,128)(2,1)}, bf16[1,768,384]{2,1,0:T(8,128)(2,1)}, u32[]{:S(2)}, u32[]{:S(2)}) collective-permute-start(bf16[1,768,384]{2,1,0:T(8,128)(2,1)} %get-tuple-element.126), channel_id=1, source_target_pairs={{0,8},{8,16},{16,24},{24,0},{1,9},{9,17},{17,25},{25,1},{2,10},{10... | collective-permute-start | bytes 1769480 | tf_op jit(solution)/shard_map/ppermute | solution.py:488
  508.8 53.5 %collective-permute-start.25 = (bf16[1,768,384]{2,1,0:T(8,128)(2,1)}, bf16[1,768,384]{2,1,0:T(8,128)(2,1)}, u32[]{:S(2)}, u32[]{:S(2)}) collective-permute-start(bf16[1,768,384]{2,1,0:T(8,128)(2,1)} %get-tuple-element.127), channel_id=1, source_target_pairs={{0,24},{8,0},{16,8},{24,16},{1,25},{9,1},{17,9},{25,17},{2,26},{10... | collective-permute-start | bytes 1769480 | tf_op jit(solution)/shard_map/ppermute | solution.py:491
  511.5 50.8 %collective-permute-start.26 = (bf16[1,384,768]{2,1,0:T(8,128)(2,1)}, bf16[1,384,768]{2,1,0:T(8,128)(2,1)}, u32[]{:S(2)}, u32[]{:S(2)}) collective-permute-start(bf16[1,384,768]{2,1,0:T(8,128)(2,1)} %get-tuple-element.128), channel_id=1, source_target_pairs={{0,8},{8,16},{16,24},{24,0},{1,9},{9,17},{17,25},{25,1},{2,10},{10... | collective-permute-start | bytes 1769480 | tf_op jit(solution)/shard_map/ppermute | solution.py:488
  548.4 16.6 %collective-permute-start.27 = (bf16[1,384,768]{2,1,0:T(8,128)(2,1)S(1)}, bf16[1,384,768]{2,1,0:T(8,128)(2,1)S(1)}, u32[]{:S(2)}, u32[]{:S(2)}) collective-permute-start(bf16[1,384,768]{2,1,0:T(8,128)(2,1)S(1)} %copy-done.22), channel_id=1, source_target_pairs={{0,24},{8,0},{16,8},{24,16},{1,25},{9,1},{17,9},{25,17},{2,26},{10... | collective-permute-start | bytes 1769480 | tf_op jit(solution)/shard_map/ppermute | solution.py:491
  551.0 13.9 %collective-permute-start.36 = (bf16[1,768,384]{2,1,0:T(8,128)(2,1)S(1)}, bf16[1,768,384]{2,1,0:T(8,128)(2,1)S(1)}, u32[]{:S(2)}, u32[]{:S(2)}) collective-permute-start(bf16[1,768,384]{2,1,0:T(8,128)(2,1)S(1)} %copy-done.21), channel_id=1, source_target_pairs={{0,8},{8,16},{16,24},{24,0},{1,9},{9,17},{17,25},{25,1},{2,10},{10... | collective-permute-start | bytes 1769480 | tf_op jit(solution)/shard_map/ppermute | solution.py:488
  559.6 25.9 %collective-permute-start.37 = (bf16[1,768,384]{2,1,0:T(8,128)(2,1)}, bf16[1,768,384]{2,1,0:T(8,128)(2,1)}, u32[]{:S(2)}, u32[]{:S(2)}) collective-permute-start(bf16[1,768,384]{2,1,0:T(8,128)(2,1)} %get-tuple-element.134), channel_id=1, source_target_pairs={{0,24},{8,0},{16,8},{24,16},{1,25},{9,1},{17,9},{25,17},{2,26},{10... | collective-permute-start | bytes 1769480 | tf_op jit(solution)/shard_map/ppermute | solution.py:491
  562.3 23.2 %collective-permute-start.38 = (bf16[1,768,384]{2,1,0:T(8,128)(2,1)}, bf16[1,768,384]{2,1,0:T(8,128)(2,1)}, u32[]{:S(2)}, u32[]{:S(2)}) collective-permute-start(bf16[1,768,384]{2,1,0:T(8,128)(2,1)} %get-tuple-element.135), channel_id=1, source_target_pairs={{0,8},{8,16},{16,24},{24,0},{1,9},{9,17},{17,25},{25,1},{2,10},{10... | collective-permute-start | bytes 1769480 | tf_op jit(solution)/shard_map/ppermute | solution.py:488
  562.3 23.3 %collective-permute-start.39 = (bf16[1,768,384]{2,1,0:T(8,128)(2,1)}, bf16[1,768,384]{2,1,0:T(8,128)(2,1)}, u32[]{:S(2)}, u32[]{:S(2)}) collective-permute-start(bf16[1,768,384]{2,1,0:T(8,128)(2,1)} %get-tuple-element.136), channel_id=1, source_target_pairs={{0,24},{8,0},{16,8},{24,16},{1,25},{9,1},{17,9},{25,17},{2,26},{10... | collective-permute-start | bytes 1769480 | tf_op jit(solution)/shard_map/ppermute | solution.py:491
  565.0 23.7 %collective-permute-start.40 = (bf16[1,384,768]{2,1,0:T(8,128)(2,1)}, bf16[1,384,768]{2,1,0:T(8,128)(2,1)}, u32[]{:S(2)}, u32[]{:S(2)}) collective-permute-start(bf16[1,384,768]{2,1,0:T(8,128)(2,1)} %get-tuple-element.137), channel_id=1, source_target_pairs={{0,8},{8,16},{16,24},{24,0},{1,9},{9,17},{17,25},{25,1},{2,10},{10... | collective-permute-start | bytes 1769480 | tf_op jit(solution)/shard_map/ppermute | solution.py:488
  566.6 31.6 %collective-permute-start.41 = (bf16[1,384,768]{2,1,0:T(8,128)(2,1)}, bf16[1,384,768]{2,1,0:T(8,128)(2,1)}, u32[]{:S(2)}, u32[]{:S(2)}) collective-permute-start(bf16[1,384,768]{2,1,0:T(8,128)(2,1)} %get-tuple-element.138), channel_id=1, source_target_pairs={{0,24},{8,0},{16,8},{24,16},{1,25},{9,1},{17,9},{25,17},{2,26},{10... | collective-permute-start | bytes 1769480 | tf_op jit(solution)/shard_map/ppermute | solution.py:491
  614.2 46.2 %all-to-all-start.3 = ((bf16[8,256,768]{2,1,0:T(8,128)(2,1)}), bf16[8,256,768]{2,1,0:T(8,128)(2,1)S(1)}, u32[]{:S(2)}, u32[]{:S(2)}) async-start(bf16[8,256,768]{2,1,0:T(8,128)(2,1)} %expert.9), calls=%async_computation.3 | async-start | bytes 6291456 | tf_op jit(solution)/shard_map/all_to_all | solution.py:605
  622.9 125.1 %reduce-scatter.5.cloned.1.call-start = ((), (), s32[]{:S(2)}) async-start(), calls=%async_computation.7 | async-start | bytes 7864320 | tf_op jit(solution)/shard_map/reduce_scatter | solution.py:611
  686.2 99.4 %all-gather.12.cloned.1.call-start = ((), (), s32[]{:S(2)}) async-start(), calls=%async_computation.10 | async-start | bytes 22560768 | tf_op jit(solution)/shard_map/all_gather | solution.py:497
  687.0 155.2 %reduce-scatter.3.cloned.1.call-start = ((), (), s32[]{:S(2)}) async-start(), calls=%async_computation.6 | async-start | bytes 7864320 | tf_op jit(solution)/shard_map/reduce_scatter | solution.py:611
  839.2 70.3 %collective-permute-start.50 = (bf16[1024,768]{1,0:T(8,128)(2,1)}, bf16[1024,768]{1,0:T(8,128)(2,1)S(1)}, u32[]{:S(2)}, u32[]{:S(2)}) collective-permute-start(bf16[1024,768]{1,0:T(8,128)(2,1)} %dense.5.refs_0_), channel_id=1, source_target_pairs={{0,8},{8,16},{16,24},{24,0},{1,9},{9,17},{17,25},{25,1},{2,10},{10... | collective-permute-start | bytes 4718600 | tf_op jit(solution)/shard_map/ppermute | solution.py:488
  840.5 72.6 %collective-permute-start.51 = (bf16[1024,768]{1,0:T(8,128)(2,1)}, bf16[1024,768]{1,0:T(8,128)(2,1)S(1)}, u32[]{:S(2)}, u32[]{:S(2)}) collective-permute-start(bf16[1024,768]{1,0:T(8,128)(2,1)} %dense.5.refs_0_), channel_id=1, source_target_pairs={{0,24},{8,0},{16,8},{24,16},{1,25},{9,1},{17,9},{25,17},{2,26},{10... | collective-permute-start | bytes 4718600 | tf_op jit(solution)/shard_map/ppermute | solution.py:491
  890.9 23.2 %collective-permute-start.46 = (bf16[512,768]{1,0:T(8,128)(2,1)}, bf16[512,768]{1,0:T(8,128)(2,1)}, u32[]{:S(2)}, u32[]{:S(2)}) collective-permute-start(bf16[512,768]{1,0:T(8,128)(2,1)} %dense.4.refs_5_), channel_id=1, source_target_pairs={{0,8},{8,16},{16,24},{24,0},{1,9},{9,17},{17,25},{25,1},{2,10},{10... | collective-permute-start | bytes 2359304 | tf_op jit(solution)/shard_map/ppermute | solution.py:488
  891.0 27.4 %collective-permute-start.47 = (bf16[512,768]{1,0:T(8,128)(2,1)}, bf16[512,768]{1,0:T(8,128)(2,1)}, u32[]{:S(2)}, u32[]{:S(2)}) collective-permute-start(bf16[512,768]{1,0:T(8,128)(2,1)} %dense.4.refs_5_), channel_id=1, source_target_pairs={{0,24},{8,0},{16,8},{24,16},{1,25},{9,1},{17,9},{25,17},{2,26},{10... | collective-permute-start | bytes 2359304 | tf_op jit(solution)/shard_map/ppermute | solution.py:491
  909.4 19.3 %collective-permute-start.42 = (bf16[512,768]{1,0:T(8,128)(2,1)}, bf16[512,768]{1,0:T(8,128)(2,1)}, u32[]{:S(2)}, u32[]{:S(2)}) collective-permute-start(bf16[512,768]{1,0:T(8,128)(2,1)} %dense.3.refs_0_), channel_id=1, source_target_pairs={{0,8},{8,16},{16,24},{24,0},{1,9},{9,17},{17,25},{25,1},{2,10},{10... | collective-permute-start | bytes 2359304 | tf_op jit(solution)/shard_map/ppermute | solution.py:488
  909.5 20.2 %collective-permute-start.43 = (bf16[512,768]{1,0:T(8,128)(2,1)}, bf16[512,768]{1,0:T(8,128)(2,1)}, u32[]{:S(2)}, u32[]{:S(2)}) collective-permute-start(bf16[512,768]{1,0:T(8,128)(2,1)} %dense.3.refs_0_), channel_id=1, source_target_pairs={{0,24},{8,0},{16,8},{24,16},{1,25},{9,1},{17,9},{25,17},{2,26},{10... | collective-permute-start | bytes 2359304 | tf_op jit(solution)/shard_map/ppermute | solution.py:491
  913.1 32.5 %collective-permute-start.52 = (bf16[512,768]{1,0:T(8,128)(2,1)}, bf16[512,768]{1,0:T(8,128)(2,1)}, u32[]{:S(2)}, u32[]{:S(2)}) collective-permute-start(bf16[512,768]{1,0:T(8,128)(2,1)} %slice.247), channel_id=1, source_target_pairs={{0,8},{8,16},{16,24},{24,0},{1,9},{9,17},{17,25},{25,1},{2,10},{10... | collective-permute-start | bytes 2359304 | tf_op jit(solution)/shard_map/ppermute | solution.py:488
  914.1 32.1 %collective-permute-start.53 = (bf16[512,768]{1,0:T(8,128)(2,1)}, bf16[512,768]{1,0:T(8,128)(2,1)}, u32[]{:S(2)}, u32[]{:S(2)}) collective-permute-start(bf16[512,768]{1,0:T(8,128)(2,1)} %slice.248), channel_id=1, source_target_pairs={{0,24},{8,0},{16,8},{24,16},{1,25},{9,1},{17,9},{25,17},{2,26},{10... | collective-permute-start | bytes 2359304 | tf_op jit(solution)/shard_map/ppermute | solution.py:491
  918.5 35.4 %collective-permute-start.48 = (bf16[256,768]{1,0:T(8,128)(2,1)}, bf16[256,768]{1,0:T(8,128)(2,1)S(1)}, u32[]{:S(2)}, u32[]{:S(2)}) collective-permute-start(bf16[256,768]{1,0:T(8,128)(2,1)} %slice.241), channel_id=1, source_target_pairs={{0,8},{8,16},{16,24},{24,0},{1,9},{9,17},{17,25},{25,1},{2,10},{10... | collective-permute-start | bytes 1179656 | tf_op jit(solution)/shard_map/ppermute | solution.py:488
  928.7 25.2 %collective-permute-start.49 = (bf16[256,768]{1,0:T(8,128)(2,1)}, bf16[256,768]{1,0:T(8,128)(2,1)S(1)}, u32[]{:S(2)}, u32[]{:S(2)}) collective-permute-start(bf16[256,768]{1,0:T(8,128)(2,1)} %slice.242), channel_id=1, source_target_pairs={{0,24},{8,0},{16,8},{24,16},{1,25},{9,1},{17,9},{25,17},{2,26},{10... | collective-permute-start | bytes 1179656 | tf_op jit(solution)/shard_map/ppermute | solution.py:491
  929.8 32.6 %collective-permute-start.44 = (bf16[256,768]{1,0:T(8,128)(2,1)S(1)}, bf16[256,768]{1,0:T(8,128)(2,1)S(1)}, u32[]{:S(2)}, u32[]{:S(2)}) collective-permute-start(bf16[256,768]{1,0:T(8,128)(2,1)S(1)} %slice.239), channel_id=1, source_target_pairs={{0,8},{8,16},{16,24},{24,0},{1,9},{9,17},{17,25},{25,1},{2,10},{10... | collective-permute-start | bytes 1179656 | tf_op jit(solution)/shard_map/ppermute | solution.py:488
  945.6 16.8 %collective-permute-start.45 = (bf16[256,768]{1,0:T(8,128)(2,1)S(1)}, bf16[256,768]{1,0:T(8,128)(2,1)S(1)}, u32[]{:S(2)}, u32[]{:S(2)}) collective-permute-start(bf16[256,768]{1,0:T(8,128)(2,1)S(1)} %slice.240), channel_id=1, source_target_pairs={{0,24},{8,0},{16,8},{24,16},{1,25},{9,1},{17,9},{25,17},{2,26},{10... | collective-permute-start | bytes 1179656 | tf_op jit(solution)/shard_map/ppermute | solution.py:491
  (37 other events, 272.0 us)
Sparse Core Ops, SparseCore 0:
  27.2 42.2 all-gather.7
  688.6 96.8 all-gather.11
Sparse Core Ops, SparseCore 1:
  257.3 53.0 all-gather.9
  686.3 61.7 reduce-scatter.4
  750.2 61.1 reduce-scatter.2
